TPU v7x, 16 devices: a whole 2x2x2 slice. The times are simulated.
16 devices in a mesh: dp: 2 (over z), stage: 2 (over y), tp: 4 (over x, core).
Axes of the slice: x: 2, y: 2, z: 2, core: 2. Of those that a mesh axis runs over, the one named last changes fastest.
Arguments:
- act_in: bfloat16 [2, 16, 28, 28, 512], P('stage', ('dp', 'tp'))
- conv_w: bfloat16 [2, 3, 3, 512, 1024], P('stage', None, None, 'tp')
- scale_vec: float32 [2, 1024], P('stage', 'tp')
- shift_vec: float32 [2, 1024], P('stage', 'tp')
- grad_z: bfloat16 [2, 16, 28, 28, 1024], P('stage', 'dp', None, None, 'tp')
Outputs:
- output 1: bfloat16 [2, 16, 28, 28, 1024], P('stage', 'dp', None, None, 'tp')
- output 2: bfloat16 [2, 16, 28, 28, 512], P('stage', ('dp', 'tp'))
- output 3: float32 [2, 3, 3, 512, 1024], P('stage', None, None, 'tp')
All inputs are finite; a program needn't handle non-finite values.
Results may differ from a plain program's by a relative error of at most 0.00419.
Values are sent between devices in bfloat16 or wider.
A program may use at most 1 GiB of HBM per device.

v0:
```python
import jax
import jax.numpy as jnp
from jax import lax
from jax.sharding import PartitionSpec as P


def conv_forward(images, kernel):
    return lax.conv_general_dilated(images, kernel, (1, 1), "SAME", dimension_numbers=("NHWC", "HWIO", "NHWC"), preferred_element_type=jnp.float32)


def conv_input_grad(grad_out, kernel):
    return lax.conv_general_dilated(grad_out, kernel[::-1, ::-1], (1, 1), "SAME", dimension_numbers=("NHWC", "HWOI", "NHWC"), preferred_element_type=jnp.float32)


def conv_kernel_grad(images, grad_out):
    return lax.conv_general_dilated(images, grad_out, (1, 1), ((1, 1), (1, 1)), dimension_numbers=("CHWN", "IHWO", "HWNC"), preferred_element_type=jnp.float32)


def solution(mesh):
    def body(act_loc, w_loc, scale_loc, shift_loc, grad_loc):
        images = act_loc[0]
        moved = lax.all_to_all(images, "tp", 3, 0, tiled=True)
        act_blk = lax.ppermute(moved, "stage", perm=[(0, 1)])
        kernel = w_loc[0]
        part_sum = conv_forward(act_blk, kernel)
        pre_out = lax.psum_scatter(part_sum, "tp", scatter_dimension=3, tiled=True)
        lin_out = pre_out * scale_loc[0] + shift_loc[0]
        z_blk = jnp.maximum(lin_out, 0.0).astype(jnp.bfloat16)
        grad_blk = jnp.where(lin_out > 0, grad_loc[0].astype(jnp.float32) * scale_loc[0], 0.0).astype(jnp.bfloat16)
        grad_full = lax.all_gather(grad_blk, "tp", axis=3, tiled=True)
        dact_blk = conv_input_grad(grad_full, kernel).astype(jnp.bfloat16)
        dw_part = conv_kernel_grad(act_blk, grad_full)
        dw_blk = lax.psum(dw_part, "dp")
        dact_back = lax.ppermute(dact_blk, "stage", perm=[(1, 0)])
        dact_img = lax.all_to_all(dact_back, "tp", 0, 3, tiled=True)
        return z_blk[None], dact_img[None], dw_blk[None]

    act_spec = P("stage", ("dp", "tp"))
    w_spec = P("stage", None, None, "tp")
    vec_spec = P("stage", "tp")
    grad_spec = P("stage", "dp", None, None, "tp")
    return jax.shard_map(body, mesh=mesh, in_specs=(act_spec, w_spec, vec_spec, vec_spec, grad_spec), out_specs=(grad_spec, act_spec, w_spec), check_vma=False)
```

profile of v0, /device:TPU:4, one launch (start us, length us, event | category | flops | bytes accessed | tf_op | source)
XLA Modules:
  0.0 594.1 jit_solution(9859013089404608174)
XLA Ops:
  7.2 0.0 copy-start
  7.2 0.0 reduce-scatter.2.cloned.1.call-start
  7.2 17.7 %copy.14 = bf16[1,2,28,28,512]{3,1,2,4,0:T(2,128)(2,1)} copy(bf16[1,2,28,28,512]{4,1,3,2,0:T(2,128)(2,1)} %param.5) | data formatting | bytes 3211264 | tf_op args[0]
  24.9 7.5 %bitcast_bitcast_fusion = bf16[512,28,2,28]{3,2,1,0:T(2,128)(2,1)} fusion(bf16[1,2,28,28,512]{3,1,2,4,0:T(2,128)(2,1)} %copy.14), kind=kLoop, calls=%fused_computation.12 | loop fusion | bytes 3211264
  32.4 18.6 %reshape.12 = bf16[4,2,100352]{2,1,0:T(2,128)(2,1)} reshape(bf16[512,28,2,28]{3,2,1,0:T(2,128)(2,1)} %bitcast_bitcast_fusion) | data formatting | bytes 3211264
  51.0 24.5 %all_to_all.33 = bf16[4,2,100352]{2,1,0:T(2,128)(2,1)} all-to-all(bf16[4,2,100352]{2,1,0:T(2,128)(2,1)} %reshape.12), channel_id=1, replica_groups=mesh['dp'=2,'stage'=2,'tp'=4] {'tp'}, dimensions={0} | all-to-all | bytes 3211264 | tf_op jit(solution)/shard_map/all_to_all | solution.py:22
  75.5 21.7 %reshape.13 = bf16[512,28,2,28]{3,2,1,0:T(2,128)(2,1)} reshape(bf16[4,2,100352]{2,1,0:T(2,128)(2,1)} %all_to_all.33) | data formatting | bytes 3211264
  97.2 18.1 %copy.15 = bf16[2,28,28,4,128]{4,0,3,2,1:T(2,128)(2,1)} copy(bf16[2,28,28,4,128]{2,0,1,4,3:T(2,128)(2,1)} %bitcast.34) | data formatting | bytes 3211264 | tf_op jit(solution)/shard_map/all_to_all | solution.py:22
  115.3 1.5 collective-permute-start
  116.8 37.5 %collective-permute-done = bf16[8,28,28,128]{3,0,2,1:T(8,128)(2,1)S(1)} collective-permute-done((bf16[8,28,28,128]{3,0,2,1:T(8,128)(2,1)}, bf16[8,28,28,128]{3,0,2,1:T(8,128)(2,1)S(1)}, u32[]{:S(2)}, u32[]{:S(2)}) %collective-permute-start) | collective-permute-done | bytes 1605664 | tf_op jit(solution)/shard_map/ppermute | solution.py:23
  154.3 0.0 copy-start.3
  154.3 1.2 copy-done.3
  155.4 0.0 copy-done
  155.4 20.1 %fusion.5 = f32[8,28,28,1024]{3,0,2,1:T(8,128)} fusion(bf16[8,28,28,128]{3,0,2,1:T(8,128)(2,1)S(1)} %collective-permute-done, bf16[1,3,3,128,1024]{4,3,2,1,0:T(8,128)(2,1)S(1)} %copy-done), kind=kOutput, calls=%fused_computation.8 | convolution fusion | flops 14101250048 | bytes 29655040 | tf_op jit(solution)/shard_map/conv_general_dilated | solution.py:8
  175.5 0.0 copy-start.1
  175.5 0.0 copy-start.2
  175.5 0.0 reduce-scatter.2.cloned.1.call-update
  175.5 0.0 all-gather.2.cloned.1.call-start
  175.6 174.2 %reduce-scatter.2.cloned.1.call-done = f32[8,28,28,256]{3,0,2,1:T(8,128)} async-done(((f32[8,28,28,1024]{3,0,2,1:T(8,128)}), f32[8,28,28,256]{3,0,2,1:T(8,128)}) %reduce-scatter.2.cloned.1.call-update) | async-done | bytes 6422544 | tf_op jit(solution)/shard_map/reduce_scatter | solution.py:26
  349.8 0.0 copy-done.1
  349.8 0.0 copy-done.2
  349.8 6.4 %fusion.1 = (bf16[8,28,28,256]{3,0,2,1:T(8,128)(2,1)}, bf16[1,8,28,28,256]{4,1,3,2,0:T(8,128)(2,1)}) fusion(f32[8,28,28,256]{3,0,2,1:T(8,128)} %reduce-scatter.2.cloned.1.call-done, bf16[1,8,28,28,256]{4,1,3,2,0:T(8,128)(2,1)} %param.9, f32[256]{0:T(256)S(1)} %bitcast.37, f32[256]{0:T(256)S(1)} %bitcast.38), kind=kLoop, calls=%fused_computation.2 | loop fusion | flops 14450688 | bytes 16058368 | tf_op jit(solution)/shard_map/convert_element_type | solution.py:29
  356.2 0.0 all-gather.2.cloned.1.call-update
  356.2 0.0 all-reduce.2.cloned.1.call-start
  356.3 84.2 %all-gather.2.cloned.1.call-done = bf16[8,28,28,1024]{3,0,2,1:T(8,128)(2,1)} async-done(((bf16[8,28,28,256]{3,0,2,1:T(8,128)(2,1)}), bf16[8,28,28,1024]{3,0,2,1:T(8,128)(2,1)}) %all-gather.2.cloned.1.call-update) | async-done | bytes 12845072 | tf_op jit(solution)/shard_map/all_gather | solution.py:30
  440.5 26.4 %convolution_bitcast_fusion = f32[1,3,3,128,1024]{4,3,2,1,0:T(8,128)} fusion(bf16[8,28,28,128]{3,0,2,1:T(8,128)(2,1)} %copy-done.3, bf16[8,28,28,1024]{3,0,2,1:T(8,128)(2,1)} %all-gather.2.cloned.1.call-done), kind=kOutput, calls=%fused_computation.10 | convolution fusion | flops 14101250048 | bytes 19169280 | tf_op jit(solution)/shard_map/conv_general_dilated | solution.py:16
  466.9 0.0 all-reduce.2.cloned.1.call-update
  466.9 33.1 %fusion.7 = bf16[8,28,28,128]{3,0,2,1:T(8,128)(2,1)S(1)} fusion(bf16[8,28,28,1024]{3,0,2,1:T(8,128)(2,1)} %all-gather.2.cloned.1.call-done, bf16[1,3,3,128,1024]{4,3,2,1,0:T(8,128)(2,1)S(1)} %copy-done), kind=kOutput, calls=%fused_computation.11 | convolution fusion | flops 14102052864 | bytes 16809984 | tf_op jit(solution)/shard_map/conv_general_dilated | solution.py:12
  500.0 2.6 collective-permute-start.1
  502.6 34.6 %collective-permute-done.1 = bf16[8,28,28,128]{3,0,2,1:T(8,128)(2,1)S(1)} collective-permute-done((bf16[8,28,28,128]{3,0,2,1:T(8,128)(2,1)S(1)}, bf16[8,28,28,128]{3,0,2,1:T(8,128)(2,1)S(1)}, u32[]{:S(2)}, u32[]{:S(2)}) %collective-permute-start.1) | collective-permute-done | bytes 1605664 | tf_op jit(solution)/shard_map/ppermute | solution.py:34
  537.2 0.3 copy.16
  537.6 25.3 %all_to_all.34 = bf16[8,28,28,128]{3,2,1,0:T(8,128)(2,1)S(1)} all-to-all(bf16[8,28,28,128]{3,2,1,0:T(8,128)(2,1)S(1)} %copy.16), channel_id=1, replica_groups=mesh['dp'=2,'stage'=2,'tp'=4] {'tp'}, dimensions={0} | all-to-all | bytes 3211264 | tf_op jit(solution)/shard_map/all_to_all | solution.py:35
  562.9 2.4 copy.17
  565.3 4.5 broadcast_in_dim.12
  569.8 12.5 %all-reduce.2.cloned.1.call-done = f32[1,3,3,128,1024]{4,3,2,1,0:T(8,128)} async-done(((f32[1,3,3,128,1024]{4,3,2,1,0:T(8,128)}), f32[1,3,3,128,1024]{4,3,2,1,0:T(8,128)}) %all-reduce.2.cloned.1.call-update) | async-done | bytes 4718608 | tf_op jit(solution)/shard_map/psum | solution.py:33
  582.3 5.2 copy.19
Async XLA Ops:
  7.2 148.3 %copy-start = (bf16[1,3,3,128,1024]{4,3,2,1,0:T(8,128)(2,1)S(1)}, bf16[1,3,3,128,1024]{4,3,2,1,0:T(8,128)(2,1)}, u32[]{:S(2)}) copy-start(bf16[1,3,3,128,1024]{4,3,2,1,0:T(8,128)(2,1)} %param.6) | copy-start | bytes 7077892
  7.2 342.6 %reduce-scatter.2.cloned.1.call-start = ((), (), s32[]{:S(2)}) async-start(), calls=%async_computation.3 | async-start | bytes 32112640 | tf_op jit(solution)/shard_map/reduce_scatter | solution.py:26
  115.3 38.9 %collective-permute-start = (bf16[8,28,28,128]{3,0,2,1:T(8,128)(2,1)}, bf16[8,28,28,128]{3,0,2,1:T(8,128)(2,1)S(1)}, u32[]{:S(2)}, u32[]{:S(2)}) collective-permute-start(bf16[8,28,28,128]{3,0,2,1:T(8,128)(2,1)} %bitcast.36), channel_id=1, source_target_pairs={{0,4},{1,5},{2,6},{3,7},{8,12},{9,13},{10,14},{11,15}} | collective-permute-start | bytes 4816904 | tf_op jit(solution)/shard_map/ppermute | solution.py:23
  154.3 1.2 copy-start.3
  175.5 174.3 %copy-start.1 = (f32[1,256]{1,0:T(1,128)S(1)}, f32[1,256]{1,0:T(1,128)}, u32[]{:S(2)}) copy-start(f32[1,256]{1,0:T(1,128)} %param.8) | copy-start | bytes 3076
  175.5 174.3 %copy-start.2 = (f32[1,256]{1,0:T(1,128)S(1)}, f32[1,256]{1,0:T(1,128)}, u32[]{:S(2)}) copy-start(f32[1,256]{1,0:T(1,128)} %param.7) | copy-start | bytes 3076
  175.5 264.9 %all-gather.2.cloned.1.call-start = ((), (), s32[]{:S(2)}) async-start(), calls=%async_computation.4 | async-start | bytes 16056320 | tf_op jit(solution)/shard_map/all_gather | solution.py:30
  356.2 226.1 %all-reduce.2.cloned.1.call-start = ((), (), s32[]{:S(2)}) async-start(), calls=%async_computation.5 | async-start | bytes 9437184 | tf_op jit(solution)/shard_map/psum | solution.py:33
  500.0 37.2 %collective-permute-start.1 = (bf16[8,28,28,128]{3,0,2,1:T(8,128)(2,1)S(1)}, bf16[8,28,28,128]{3,0,2,1:T(8,128)(2,1)S(1)}, u32[]{:S(2)}, u32[]{:S(2)}) collective-permute-start(bf16[8,28,28,128]{3,0,2,1:T(8,128)(2,1)S(1)} %fusion.7), channel_id=1, source_target_pairs={{4,0},{5,1},{6,2},{7,3},{12,8},{13,9},{14,10},{15,11}} | collective-permute-start | bytes 4816904 | tf_op jit(solution)/shard_map/ppermute | solution.py:34
Sparse Core Ops, SparseCore 0:
  175.7 174.0 reduce-scatter.1
  356.3 84.0 all-gather.1
  467.0 115.2 all-reduce.1
where the time goes:
time: 598 us; the launch traced here: 594 us
  waiting for transfers between devices  343 us (57%)
  local copies, waits for them, and re-layouts  97.2 us (16%)
  matrix products  79.6 us (13%)
  blocking collectives  49.8 us (8%)
  between operations  13.8 us (2%)
  other arithmetic  6.41 us (1%)
    reduce_scatter x1, waiting for transfers between devices, body(): pre_out = lax.psum_scatter(part_sum, 'tp', scatter_dimension=3, tiled=True)  174 us
    all_gather x1, waiting for transfers between devices, body(): grad_full = lax.all_gather(grad_blk, 'tp', axis=3, tiled=True)  84.2 us
    unnamed x13, local copies, waits for them, and re-layouts  71.9 us
    ppermute x1, waiting for transfers between devices, body(): act_blk = lax.ppermute(moved, 'stage', perm=[(0, 1)])  37.5 us
    ppermute x1, waiting for transfers between devices, body(): dact_back = lax.ppermute(dact_blk, 'stage', perm=[(1, 0)])  34.6 us
    conv_general_dilated x1, matrix products, conv_input_grad(): lax.conv_general_dilated(grad_out, kernel[::-1, ::-1], (1, 1), 'SAME', di...  33.1 us
    conv_general_dilated x1, matrix products, conv_kernel_grad(): lax.conv_general_dilated(images, grad_out, (1, 1), ((1, 1), (1, 1)), dime...  26.4 us
    all_to_all x1, blocking collectives, body(): dact_img = lax.all_to_all(dact_back, 'tp', 0, 3, tiled=True)  25.3 us
  transfers between devices with their start and end apart: 5, of which 5 were waited for; matrix products, arithmetic and copies ran while one was open for 7% of the time, Pallas kernels for 0%

commit v1 on v0

--- a/solution.py
+++ b/solution.py
@@ -18,19 +18,20 @@
 
 def solution(mesh):
     def body(act_loc, w_loc, scale_loc, shift_loc, grad_loc):
-        images = act_loc[0]
-        moved = lax.all_to_all(images, "tp", 3, 0, tiled=True)
-        act_blk = lax.ppermute(moved, "stage", perm=[(0, 1)])
         kernel = w_loc[0]
-        part_sum = conv_forward(act_blk, kernel)
-        pre_out = lax.psum_scatter(part_sum, "tp", scatter_dimension=3, tiled=True)
+        kern_out = lax.all_to_all(kernel, "tp", 3, 2, tiled=True)
+        moved = lax.ppermute(act_loc[0], "stage", perm=[(0, 1)])
+        act_all = lax.all_gather(moved, "tp", axis=0, tiled=True)
+        pre_out = conv_forward(act_all, kern_out)
         lin_out = pre_out * scale_loc[0] + shift_loc[0]
         z_blk = jnp.maximum(lin_out, 0.0).astype(jnp.bfloat16)
         grad_blk = jnp.where(lin_out > 0, grad_loc[0].astype(jnp.float32) * scale_loc[0], 0.0).astype(jnp.bfloat16)
         grad_full = lax.all_gather(grad_blk, "tp", axis=3, tiled=True)
-        dact_blk = conv_input_grad(grad_full, kernel).astype(jnp.bfloat16)
+        tp_idx = lax.axis_index("tp")
+        act_blk = lax.dynamic_slice_in_dim(act_all, tp_idx * 128, 128, axis=3)
         dw_part = conv_kernel_grad(act_blk, grad_full)
         dw_blk = lax.psum(dw_part, "dp")
+        dact_blk = conv_input_grad(grad_full, kernel).astype(jnp.bfloat16)
         dact_back = lax.ppermute(dact_blk, "stage", perm=[(1, 0)])
         dact_img = lax.all_to_all(dact_back, "tp", 0, 3, tiled=True)
         return z_blk[None], dact_img[None], dw_blk[None]

time: 598 us -> 400 us (0.67)
  waiting for transfers between devices: 343 us -> 170 us
  local copies, waits for them, and re-layouts: 97.2 us -> 32.3 us
  blocking collectives: 49.8 us -> 99.5 us
  other arithmetic: 6.41 us -> 0 us
    reduce_scatter x1 -> x0, waiting for transfers between devices: 174 us -> none  [body(): pre_out = lax.psum_scatter(part_sum, 'tp', scatter_dimension=3, tiled=True)]
    unnamed x13 -> x12, local copies, waits for them, and re-layouts: 71.9 us -> 10.1 us
    all_to_all x1, blocking collectives: 24.5 us -> 74.2 us  [body(): kern_out = lax.all_to_all(kernel, 'tp', 3, 2, tiled=True)]
    all_to_all x1, local copies, waits for them, and re-layouts: 18.1 us -> 5.61 us  [body(): kern_out = lax.all_to_all(kernel, 'tp', 3, 2, tiled=True)]
    all_gather x0 -> x1, local copies, waits for them, and re-layouts: none -> 7.8 us  [body(): act_all = lax.all_gather(moved, 'tp', axis=0, tiled=True)]
    convert_element_type x1 -> x0, other arithmetic: 6.41 us -> none  [body(): jnp.where(lin_out > 0, grad_loc[0].astype(jnp.float32) * scale_loc[0], 0.0)]
  transfers between devices with their start and end apart: 5 -> 5, of which waited for: 5 -> 5; matrix products, arithmetic and copies ran while one was open for 7% -> 13% of each run, Pallas kernels for 0% -> 0%
where the time goes in v1:
time: 400 us; the launch traced here: 397 us
  waiting for transfers between devices  170 us (42%)
  blocking collectives  99.5 us (25%)
  matrix products  78 us (20%)
  local copies, waits for them, and re-layouts  32.3 us (8%)
  between operations  13.8 us (3%)
  starting transfers between devices  4.17 us (1%)
    all_gather x1, waiting for transfers between devices, body(): grad_full = lax.all_gather(grad_blk, 'tp', axis=3, tiled=True)  84 us
    all_to_all x1, blocking collectives, body(): kern_out = lax.all_to_all(kernel, 'tp', 3, 2, tiled=True)  74.2 us
    ppermute x1, waiting for transfers between devices, body(): moved = lax.ppermute(act_loc[0], 'stage', perm=[(0, 1)])  37.4 us
    ppermute x1, waiting for transfers between devices, body(): dact_back = lax.ppermute(dact_blk, 'stage', perm=[(1, 0)])  34.6 us
    conv_general_dilated x1, matrix products, conv_input_grad(): lax.conv_general_dilated(grad_out, kernel[::-1, ::-1], (1, 1), 'SAME', di...  32.9 us
    conv_general_dilated x1, matrix products, conv_kernel_grad(): lax.conv_general_dilated(images, grad_out, (1, 1), ((1, 1), (1, 1)), dime...  26.5 us
    all_to_all x1, blocking collectives, body(): dact_img = lax.all_to_all(dact_back, 'tp', 0, 3, tiled=True)  25.3 us
    conv_general_dilated x1, matrix products, conv_forward(): lax.conv_general_dilated(images, kernel, (1, 1), 'SAME', dimension_number...  18.6 us
  transfers between devices with their start and end apart: 5, of which 5 were waited for; matrix products, arithmetic and copies ran while one was open for 13% of the time, Pallas kernels for 0%

profile of v1, /device:TPU:4, one launch (start us, length us, event | category | flops | bytes accessed | tf_op | source)
XLA Modules:
  0.0 397.4 jit_solution(2610957032111794267)
XLA Ops:
  7.2 0.0 all-gather.3.cloned.1.call-start
  7.2 1.3 collective-permute-start
  8.5 37.4 %collective-permute-done = bf16[2,28,28,512]{3,0,2,1:T(2,128)(2,1)S(1)} collective-permute-done((bf16[2,28,28,512]{3,0,2,1:T(2,128)(2,1)}, bf16[2,28,28,512]{3,0,2,1:T(2,128)(2,1)S(1)}, u32[]{:S(2)}, u32[]{:S(2)}) %collective-permute-start) | collective-permute-done | bytes 1605664 | tf_op jit(solution)/shard_map/ppermute | solution.py:23
  45.9 1.6 copy.18
  47.6 0.0 all-gather.3.cloned.1.call-update
  47.6 0.0 all-gather.5.cloned.1.call-start
  47.6 4.8 %copy.19 = bf16[1,3,3,128,1024]{3,2,1,4,0:T(4,128)(2,1)S(1)} copy(bf16[1,3,3,128,1024]{4,3,2,1,0:T(8,128)(2,1)} %param.6) | data formatting | bytes 4718592 | tf_op args[1]
  52.5 74.2 %all_to_all.33 = bf16[3,3,128,1024]{2,1,0,3:T(4,128)(2,1)} all-to-all(bf16[3,3,128,1024]{2,1,0,3:T(4,128)(2,1)S(1)} %bitcast.24), channel_id=1, replica_groups=mesh['dp'=2,'stage'=2,'tp'=4] {'tp'}, dimensions={3} | all-to-all | bytes 4718592 | tf_op jit(solution)/shard_map/all_to_all | solution.py:22
  126.7 5.6 %copy.20 = bf16[3,3,128,4,256]{4,2,3,1,0:T(8,128)(2,1)} copy(bf16[3,3,128,4,256]{2,1,0,4,3:T(4,128)(2,1)} %bitcast.26) | data formatting | bytes 4718592 | tf_op jit(solution)/shard_map/all_to_all | solution.py:22
  132.3 0.0 copy-start.3
  132.3 0.0 copy-start.4
  132.3 0.7 all-gather.3.cloned.1.call-done
  133.1 0.0 copy-start.1
  133.1 0.0 copy-start.2
  133.1 7.8 %copy.21 = bf16[8,28,28,512]{3,0,2,1:T(8,128)(2,1)S(1)} copy(bf16[8,28,28,512]{3,2,1,0:T(8,128)(2,1)} %all-gather.3.cloned.1.call-done) | data formatting | bytes 12845056 | tf_op jit(solution)/shard_map/all_gather | solution.py:24
  140.9 0.0 copy-start
  140.9 0.0 copy-done.3
  140.9 0.0 copy-done.4
  140.9 0.0 copy-done.1
  140.9 0.0 copy-done.2
  140.9 18.6 %fusion.1 = (bf16[8,28,28,256]{3,0,2,1:T(8,128)(2,1)}, bf16[1,8,28,28,256]{4,1,3,2,0:T(8,128)(2,1)}) fusion(bf16[1,8,28,28,256]{4,1,3,2,0:T(8,128)(2,1)S(1)} %copy-done.2, f32[256]{0:T(256)S(1)} %bitcast.30, f32[256]{0:T(256)S(1)} %bitcast.31, bf16[8,28,28,512]{3,0,2,1:T(8,128)(2,1)S(1)} %copy.21, bf16[3,3,512,256]{3,2,1,0:T(8,128)(2,1)S(1)} %bitcast.28), kind=kOutput, calls=%fused_computation.2 | convolution fusion | flops 14115700736 | bytes 18417664 | tf_op jit(solution)/shard_map/conv_general_dilated | solution.py:8
  159.5 0.0 copy-done
  159.5 0.0 all-gather.5.cloned.1.call-update
  159.6 0.2 all-reduce.2.cloned.1.call-start
  159.8 84.0 %all-gather.5.cloned.1.call-done = bf16[8,28,28,1024]{3,0,2,1:T(8,128)(2,1)} async-done(((bf16[8,28,28,256]{3,0,2,1:T(8,128)(2,1)}), bf16[8,28,28,1024]{3,0,2,1:T(8,128)(2,1)}) %all-gather.5.cloned.1.call-update) | async-done | bytes 12845072 | tf_op jit(solution)/shard_map/all_gather | solution.py:29
  243.8 26.5 %convolution_bitcast_fusion = f32[1,3,3,128,1024]{4,3,2,1,0:T(8,128)} fusion(bf16[8,28,28,1024]{3,0,2,1:T(8,128)(2,1)} %all-gather.5.cloned.1.call-done, bf16[8,28,28,512]{3,0,2,1:T(8,128)(2,1)} %copy-done, s32[]{:T(128)S(6)} %select_n.8), kind=kOutput, calls=%fused_computation.8 | convolution fusion | flops 14101250048 | bytes 19169284 | tf_op jit(solution)/shard_map/conv_general_dilated | solution.py:16
  270.3 0.0 all-reduce.2.cloned.1.call-update
  270.3 32.9 %fusion.5 = bf16[8,28,28,128]{3,0,2,1:T(8,128)(2,1)S(1)} fusion(bf16[8,28,28,1024]{3,0,2,1:T(8,128)(2,1)} %all-gather.5.cloned.1.call-done, bf16[3,3,128,1024]{2,1,0,3:T(4,128)(2,1)S(1)} %bitcast.25), kind=kOutput, calls=%fused_computation.9 | convolution fusion | flops 14102052864 | bytes 16809984 | tf_op jit(solution)/shard_map/conv_general_dilated | solution.py:12
  303.2 2.6 collective-permute-start.1
  305.8 34.6 %collective-permute-done.1 = bf16[8,28,28,128]{3,0,2,1:T(8,128)(2,1)S(1)} collective-permute-done((bf16[8,28,28,128]{3,0,2,1:T(8,128)(2,1)S(1)}, bf16[8,28,28,128]{3,0,2,1:T(8,128)(2,1)S(1)}, u32[]{:S(2)}, u32[]{:S(2)}) %collective-permute-start.1) | collective-permute-done | bytes 1605664 | tf_op jit(solution)/shard_map/ppermute | solution.py:35
  340.4 0.3 copy.23
  340.7 25.3 %all_to_all.34 = bf16[8,28,28,128]{3,2,1,0:T(8,128)(2,1)S(1)} all-to-all(bf16[8,28,28,128]{3,2,1,0:T(8,128)(2,1)S(1)} %copy.23), channel_id=1, replica_groups=mesh['dp'=2,'stage'=2,'tp'=4] {'tp'}, dimensions={0} | all-to-all | bytes 3211264 | tf_op jit(solution)/shard_map/all_to_all | solution.py:36
  366.0 2.4 copy.24
  368.5 4.5 %broadcast_in_dim.12 = bf16[1,2,28,28,512]{4,1,3,2,0:T(2,128)(2,1)} reshape(bf16[2,28,28,4,128]{4,3,0,2,1:T(4,128)(2,1)} %copy.24) | data formatting | bytes 3211264 | tf_op jit(solution)/shard_map/broadcast_in_dim | solution.py:37
  372.9 12.7 %all-reduce.2.cloned.1.call-done = f32[1,3,3,128,1024]{4,3,2,1,0:T(8,128)} async-done(((f32[1,3,3,128,1024]{4,3,2,1,0:T(8,128)}), f32[1,3,3,128,1024]{4,3,2,1,0:T(8,128)}) %all-reduce.2.cloned.1.call-update) | async-done | bytes 4718608 | tf_op jit(solution)/shard_map/psum | solution.py:33
  385.7 5.2 %copy.31 = f32[1,3,3,128,1024]{4,3,2,1,0:T(8,128)} copy(f32[1,3,3,128,1024]{4,3,2,1,0:T(8,128)} %all-reduce.2.cloned.1.call-done) | data formatting | bytes 9437184
Async XLA Ops:
  7.2 125.9 %all-gather.3.cloned.1.call-start = ((), (), s32[]{:S(2)}) async-start(), calls=%async_computation.2 | async-start | bytes 9175040 | tf_op jit(solution)/shard_map/all_gather | solution.py:24
  7.2 38.7 %collective-permute-start = (bf16[2,28,28,512]{3,0,2,1:T(2,128)(2,1)}, bf16[2,28,28,512]{3,0,2,1:T(2,128)(2,1)S(1)}, u32[]{:S(2)}, u32[]{:S(2)}) collective-permute-start(bf16[2,28,28,512]{3,0,2,1:T(2,128)(2,1)} %bitcast.29), channel_id=1, source_target_pairs={{0,4},{1,5},{2,6},{3,7},{8,12},{9,13},{10,14},{11,15}} | collective-permute-start | bytes 4816904 | tf_op jit(solution)/shard_map/ppermute | solution.py:23
  47.6 196.2 %all-gather.5.cloned.1.call-start = ((), (), s32[]{:S(2)}) async-start(), calls=%async_computation.3 | async-start | bytes 16056320 | tf_op jit(solution)/shard_map/all_gather | solution.py:29
  132.3 8.6 %copy-start.3 = (f32[1,256]{1,0:T(1,128)S(1)}, f32[1,256]{1,0:T(1,128)}, u32[]{:S(2)}) copy-start(f32[1,256]{1,0:T(1,128)} %param.8) | copy-start | bytes 3076
  132.3 8.6 %copy-start.4 = (f32[1,256]{1,0:T(1,128)S(1)}, f32[1,256]{1,0:T(1,128)}, u32[]{:S(2)}) copy-start(f32[1,256]{1,0:T(1,128)} %param.7) | copy-start | bytes 3076
  133.1 7.8 %copy-start.1 = (bf16[3,3,128,4,256]{4,2,3,1,0:T(8,128)(2,1)S(1)}, bf16[3,3,128,4,256]{4,2,3,1,0:T(8,128)(2,1)}, u32[]{:S(2)}) copy-start(bf16[3,3,128,4,256]{4,2,3,1,0:T(8,128)(2,1)} %copy.20) | copy-start | bytes 7077892
  133.1 7.8 %copy-start.2 = (bf16[1,8,28,28,256]{4,1,3,2,0:T(8,128)(2,1)S(1)}, bf16[1,8,28,28,256]{4,1,3,2,0:T(8,128)(2,1)}, u32[]{:S(2)}) copy-start(bf16[1,8,28,28,256]{4,1,3,2,0:T(8,128)(2,1)} %param.9) | copy-start | bytes 9633796
  140.9 18.7 %copy-start = (bf16[8,28,28,512]{3,0,2,1:T(8,128)(2,1)}, bf16[8,28,28,512]{3,0,2,1:T(8,128)(2,1)S(1)}, u32[]{:S(2)}) copy-start(bf16[8,28,28,512]{3,0,2,1:T(8,128)(2,1)S(1)} %copy.21) | copy-start | bytes 19267588
  159.6 226.1 %all-reduce.2.cloned.1.call-start = ((), (), s32[]{:S(2)}) async-start(), calls=%async_computation.4 | async-start | bytes 9437184 | tf_op jit(solution)/shard_map/psum | solution.py:33
  303.2 37.2 %collective-permute-start.1 = (bf16[8,28,28,128]{3,0,2,1:T(8,128)(2,1)S(1)}, bf16[8,28,28,128]{3,0,2,1:T(8,128)(2,1)S(1)}, u32[]{:S(2)}, u32[]{:S(2)}) collective-permute-start(bf16[8,28,28,128]{3,0,2,1:T(8,128)(2,1)S(1)} %fusion.5), channel_id=1, source_target_pairs={{4,0},{5,1},{6,2},{7,3},{12,8},{13,9},{14,10},{15,11}} | collective-permute-start | bytes 4816904 | tf_op jit(solution)/shard_map/ppermute | solution.py:35
Sparse Core Ops, SparseCore 0:
  47.7 85.3 all-gather.2
  159.7 84.0 all-gather.4
  270.4 115.2 all-reduce.1

commit v2 on v0

v2 whole, which is shorter than its diff:
```python
import functools

import jax
import jax.numpy as jnp
from jax import lax
from jax.experimental import pallas as pl
from jax.experimental.pallas import tpu as pltpu
from jax.sharding import PartitionSpec as P

BF = jnp.bfloat16
F32 = jnp.float32
MESH = pl.DeviceIdType.MESH
CH = 4
CR = 7


def kernel(act, w, sc, sh, gz, z_out, da_out, dw_out, A, AC, KO, KCU, KT, DZ, GU, W, WR, ACC, DAO, ZB,
           lsem, ksem_s, ksem_r, kc_s, kc_r, kc_l, as_s, a_r, f_s, g_s, g_r, zx_s, zx_r, da_s, da_r, out_s):
    dp = lax.axis_index("dp")
    stage = lax.axis_index("stage")
    t = lax.axis_index("tp")
    x = t // 2
    k = t % 2
    sib = x * 2 + (1 - k)
    xn = (1 - x) * 2 + k
    dg = (1 - x) * 2 + (1 - k)
    base = (1 - x) * 512

    def al(v, m):
        return pl.multiple_of(v, m)

    def remote(src, dst, ssem, rsem, **dev):
        return pltpu.make_async_remote_copy(src_ref=src, dst_ref=dst, send_sem=ssem, recv_sem=rsem, device_id=dev, device_id_type=MESH)

    A[0] = jnp.zeros((30, 8, 512), BF)
    A[29] = jnp.zeros((30, 8, 512), BF)
    A[:, 0] = jnp.zeros((30, 8, 512), BF)
    A[:, 29] = jnp.zeros((30, 8, 512), BF)

    def zero_halo(u, carry):
        GU[u, 0] = jnp.zeros((30, 8, 256), BF)
        GU[u, 29] = jnp.zeros((30, 8, 256), BF)
        GU[u, :, 0] = jnp.zeros((30, 8, 256), BF)
        GU[u, :, 29] = jnp.zeros((30, 8, 256), BF)
        return carry

    lax.fori_loop(0, 4, zero_halo, 0)

    barrier = pltpu.get_barrier_semaphore()
    for ds in range(2):
        for dt in range(4):
            if ds or dt:
                pl.semaphore_signal(barrier, inc=1, device_id={"stage": (stage + ds) % 2, "tp": (t + dt) % 4}, device_id_type=MESH)
    pl.semaphore_signal(barrier, inc=1, device_id={"dp": 1 - dp}, device_id_type=MESH)
    pl.semaphore_wait(barrier, 8)

    def k_copy(rel, peer, src_tp):
        return remote(w.at[:, :, pl.ds(al(256 * peer, 256), 256)], KO.at[:, pl.ds(al(128 * src_tp, 128), 128), :],
                      ksem_s.at[rel], ksem_r.at[rel], tp=peer)

    def kc_pieces(own, other):
        return ((0, 0, 256, 256 * own), (1, 0, 256, 256 * other), (2, 0, 128, base), (2, 128, 128, base + 256),
                (3, 0, 128, base + 128), (3, 128, 128, base + 384))

    def a_slot(src, c):
        return A.at[pl.ds(1 + CR * c, CR), pl.ds(1, 28), pl.ds(2 * src, 2), :]

    def a_direct(c):
        return remote(act.at[pl.ds(CR * c, CR)], a_slot(t, c), as_s.at[c], a_r.at[3, c], stage=1)

    def a_fwd(kind, c):
        if kind == 0:
            return remote(a_slot(t, c), a_slot(t, c), f_s.at[0, c], a_r.at[0, c], tp=sib)
        if kind == 1:
            return remote(a_slot(t, c), a_slot(t, c), f_s.at[1, c], a_r.at[1, c], tp=xn)
        return remote(a_slot(xn, c), a_slot(xn, c), f_s.at[2, c], a_r.at[2, c], tp=sib)

    def a_recv(rel, src, c):
        return remote(a_slot(src, c), a_slot(src, c), f_s.at[0, c], a_r.at[rel, c], tp=sib)

    def g_inner(u, lane, width):
        return GU.at[u, pl.ds(1, 28), pl.ds(1, 28), :, pl.ds(lane, width)]

    def da_copy(s, n):
        return remote(DAO.at[pl.ds(2 * n, 2), :, pl.ds(2 * s, 2), :],
                      da_out.at[pl.ds(14 * k + 2 * n, 2), :, :, pl.ds(al(256 * x, 256), 256)],
                      da_s.at[s, n], da_r.at[t, n], stage=0, tp=s)

    @pl.when(stage == 0)
    def _():
        for c in range(CH):
            a_direct(c).start()
        W[0] = jnp.zeros((9, 128, 256), F32)

        def zrow(h, carry):
            DZ[h] = jnp.zeros((28, 8, 256), BF)
            return carry

        lax.fori_loop(0, 28, zrow, 0)
        outs = [pltpu.make_async_copy(W.at[0], dw_out.at[:, :, pl.ds(256 * u, 256)], out_s.at[u]) for u in range(4)]
        outs.append(pltpu.make_async_copy(DZ, z_out, out_s.at[4]))
        for o in outs:
            o.start()
        for o in outs:
            o.wait()
        for c in range(CH):
            a_direct(c).wait_send()
        for src in range(4):
            for n in range(7):
                remote(DAO.at[pl.ds(2 * n, 2), :, pl.ds(0, 2), :],
                       da_out.at[pl.ds(14 * (src % 2) + 2 * n, 2), :, :, pl.ds(256 * (src // 2), 256)],
                       da_s.at[0, n], da_r.at[src, n], stage=0, tp=0).wait_recv()

    @pl.when(stage == 1)
    def _():
        k_copy(1, xn, t).start()
        k_copy(2, dg, t).start()
        k_copy(0, sib, t).start()
        for i, (u, lane, wd, src) in enumerate(kc_pieces(sib, t)):
            remote(w.at[:, :, pl.ds(al(src, 128), wd)], KCU.at[u, :, pl.ds(al(128 * k, 128), 128), pl.ds(lane, wd)],
                   kc_s.at[i], kc_r.at[i], tp=sib).start()
        loc = [pltpu.make_async_copy(w.at[:, :, pl.ds(al(src, 128), wd)], KCU.at[u, :, pl.ds(al(128 * k, 128), 128), pl.ds(lane, wd)], kc_l.at[i])
               for i, (u, lane, wd, src) in enumerate(kc_pieces(t, sib))]
        loc.append(pltpu.make_async_copy(w.at[:, :, pl.ds(al(256 * t, 256), 256)], KO.at[:, pl.ds(al(128 * t, 128), 128), :], lsem.at[0]))
        loc.append(pltpu.make_async_copy(gz, DZ, lsem.at[1]))
        for o in loc:
            o.start()
        ZB[...] = jnp.zeros((7, 28, 2, 512), BF)
        zcp = [pltpu.make_async_copy(ZB, da_out.at[pl.ds(7 * i, 7)], out_s.at[i]) for i in range(4)]
        for o in zcp:
            o.start()
        ACC[...] = jnp.zeros((14, 224, 256), F32)

        for c in range(CH):
            a_recv(3, t, c).wait_recv()
            a_fwd(1, c).start()
            a_fwd(0, c).start()
            if c == 0:
                for o in loc:
                    o.wait()
                for o in zcp:
                    o.wait()
                for i, (u, lane, wd, src) in enumerate(kc_pieces(t, sib)):
                    remote(w.at[:, :, pl.ds(al(src, 128), wd)], KCU.at[u, :, pl.ds(al(128 * (1 - k), 128), 128), pl.ds(lane, wd)],
                           kc_s.at[i], kc_r.at[i], tp=sib).wait_recv()

            def tr(tap, carry, c=c):
                KT[c, pl.ds(tap * 256, 256)] = KCU[c, tap].T
                return carry

            lax.fori_loop(0, 9, tr, 0)

        k_copy(1, t, xn).wait_recv()
        k_copy(2, t, dg).wait_recv()
        k_copy(0, t, sib).wait_recv()

        def chunk(c, carry):
            a_recv(1, xn, c).wait_recv()
            a_fwd(2, c).start()
            a_recv(0, sib, c).wait_recv()
            a_recv(2, dg, c).wait_recv()

            def row(h, inner):
                lhs = jnp.concatenate([A[h + i, j:j + 28].reshape(224, 512) for i in range(3) for j in range(3)], axis=1)
                pre = jnp.dot(lhs, KO[...].reshape(4608, 256), preferred_element_type=F32)
                y = pre * sc[...] + sh[...]
                d = DZ[h].reshape(224, 256).astype(F32)
                g = jnp.where(y > 0, d * sc[...], 0.0).astype(BF)
                DZ[h] = jnp.maximum(y, 0.0).astype(BF).reshape(28, 8, 256)
                GU[0, h + 1, 1:29] = g.reshape(28, 8, 256)
                return inner

            lax.fori_loop(CR * c - (c + 2) // 3, CR * (c + 1) - 1 + c // 3, row, 0)
            return carry

        lax.fori_loop(0, CH, chunk, 0)

        z_cp = pltpu.make_async_copy(DZ, z_out, lsem.at[0])
        ac_cp = pltpu.make_async_copy(A.at[:, :, :, pl.ds(al(128 * t, 128), 128)], AC, lsem.at[1])
        g_sib = remote(GU.at[0], GU.at[1], g_s.at[0], g_r.at[0], tp=sib)
        g_x = [remote(g_inner(0, 128 * q, 128), g_inner(2 + q, al(128 * k, 128), 128), g_s.at[1 + q], g_r.at[1 + q], tp=xn) for q in range(2)]
        g_rel = [remote(g_inner(2 + q, al(128 * k, 128), 128), g_inner(2 + q, al(128 * k, 128), 128), g_s.at[3 + q], g_r.at[3 + q], tp=sib) for q in range(2)]
        ac_cp.start()
        g_x[0].start()
        g_x[1].start()
        g_sib.start()
        z_cp.start()
        ac_cp.wait()

        zx = [remote(W.at[u], WR.at[u], zx_s.at[u], zx_r.at[u], dp=1 - dp) for u in range(4)]

        def dw_unit(u):
            W[u] = jnp.zeros((9, 128, 256), F32)

            def step(n, carry):
                h = n * 7
                lhs = jnp.concatenate([AC[pl.ds(h + i, 7), j:j + 28].reshape(1568, 128) for i in range(3) for j in range(3)], axis=1)
                rhs = GU[u, pl.ds(h + 1, 7), 1:29].reshape(1568, 256)
                p = lax.dot_general(lhs, rhs, (((0,), (0,)), ((), ())), preferred_element_type=F32)
                W[u] += p.reshape(9, 128, 256)
                return carry

            lax.fori_loop(0, 4, step, 0)
            zx[u].start()

        def da_rows(u, n):
            h = 14 * k + 2 * n
            lhs = jnp.concatenate([GU[u, pl.ds(h + 2 - i, 2), 2 - j:30 - j].reshape(448, 256) for i in range(3) for j in range(3)], axis=1)
            return jnp.dot(lhs, KT[u], preferred_element_type=F32)

        def da_unit(u):
            def step(n, carry):
                ACC[pl.ds(2 * n, 2)] += da_rows(u, n).reshape(2, 224, 256)
                return carry

            lax.fori_loop(0, 7, step, 0)

        dw_dst = ((256 * t,), (256 * sib,), (base, base + 256), (base + 128, base + 384))

        def dw_out_cp(u):
            starts = dw_dst[u]
            wd = 256 // len(starts)
            return [pltpu.make_async_copy(WR.at[u, :, :, pl.ds(wd * i, wd)], dw_out.at[:, :, pl.ds(al(s, 128), wd)], kc_l.at[2 * (u // 2) + (u % 2) * (u // 2) + u % 2 + i])
                    for i, s in enumerate(starts)]

        def dw_final(u):
            zx[u].wait_recv()

            def add(q, carry):
                WR[u, q] += W[u, q]
                return carry

            lax.fori_loop(0, 9, add, 0)
            for o in dw_out_cp(u):
                o.start()

        dw_unit(0)
        g_sib.wait_recv()
        dw_unit(1)
        da_unit(0)
        da_unit(1)
        for q in range(2):
            u = 2 + q
            g_x[q].wait_recv()
            g_rel[q].start()
            remote(g_inner(u, 0, 128), g_inner(u, al(128 * (1 - k), 128), 128), g_s.at[3 + q], g_r.at[3 + q], tp=sib).wait_recv()
            dw_unit(u)
            if q == 0:
                da_unit(2)
                dw_final(0)

        def last(n, carry):
            v = ACC[pl.ds(2 * n, 2)].reshape(448, 256) + da_rows(3, n)
            DAO[pl.ds(2 * n, 2)] = v.astype(BF).reshape(2, 28, 8, 256)
            for s in range(4):
                da_copy(s, n).start()
            return carry

        lax.fori_loop(0, 7, last, 0)
        for u in range(1, 4):
            dw_final(u)

        z_cp.wait()
        for u in range(4):
            for o in dw_out_cp(u):
                o.wait()
            zx[u].wait_send()
        k_copy(1, xn, t).wait_send()
        k_copy(2, dg, t).wait_send()
        k_copy(0, sib, t).wait_send()
        for i, (u, lane, wd, src) in enumerate(kc_pieces(sib, t)):
            remote(w.at[:, :, pl.ds(al(src, 128), wd)], KCU.at[u, :, pl.ds(al(128 * k, 128), 128), pl.ds(lane, wd)],
                   kc_s.at[i], kc_r.at[i], tp=sib).wait_send()
        for c in range(CH):
            for kind in range(3):
                a_fwd(kind, c).wait_send()
        g_sib.wait_send()
        for q in range(2):
            g_x[q].wait_send()
            g_rel[q].wait_send()
        for s in range(4):
            for n in range(7):
                da_copy(s, n).wait_send()


def solution(mesh):
    V = pltpu.VMEM
    D = pltpu.SemaphoreType.DMA
    any_spec = pl.BlockSpec(memory_space=pl.ANY)
    vm_spec = pl.BlockSpec(memory_space=pltpu.VMEM)
    call = pl.pallas_call(
        kernel,
        out_shape=[jax.ShapeDtypeStruct((28, 28, 8, 256), BF), jax.ShapeDtypeStruct((28, 28, 2, 512), BF), jax.ShapeDtypeStruct((9, 128, 1024), F32)],
        in_specs=[any_spec, any_spec, vm_spec, vm_spec, any_spec],
        out_specs=[any_spec] * 3,
        scratch_shapes=[
            V((30, 30, 8, 512), BF), V((30, 30, 8, 128), BF), V((9, 512, 256), BF), V((4, 9, 256, 256), BF), V((4, 2304, 256), BF),
            V((28, 28, 8, 256), BF), V((4, 30, 30, 8, 256), BF), V((4, 9, 128, 256), F32), V((4, 9, 128, 256), F32),
            V((14, 224, 256), F32), V((14, 28, 8, 256), BF), V((7, 28, 2, 512), BF),
            D((2,)), D((3,)), D((3,)), D((6,)), D((6,)), D((6,)), D((4,)), D((4, 4)), D((3, 4)), D((5,)), D((5,)), D((4,)), D((4,)),
            D((4, 7)), D((4, 7)), D((5,)),
        ],
        compiler_params=pltpu.CompilerParams(collective_id=0, has_side_effects=True, vmem_limit_bytes=66000000),
        name="conv_block",
    )

    def body(act_loc, w_loc, scale_loc, shift_loc, grad_loc):
        z, da, dw = call(act_loc[0].transpose(1, 2, 0, 3), w_loc[0].reshape(9, 128, 1024), scale_loc, shift_loc, grad_loc[0].transpose(1, 2, 0, 3))
        return z.transpose(2, 0, 1, 3)[None], da.transpose(2, 0, 1, 3)[None], dw.reshape(1, 3, 3, 128, 1024)

    act_spec = P("stage", ("dp", "tp"))
    w_spec = P("stage", None, None, "tp")
    vec_spec = P("stage", "tp")
    grad_spec = P("stage", "dp", None, None, "tp")
    return jax.shard_map(body, mesh=mesh, in_specs=(act_spec, w_spec, vec_spec, vec_spec, grad_spec), out_specs=(grad_spec, act_spec, w_spec), check_vma=False)
```

time: 598 us -> 198 us (0.33)
  waiting for transfers between devices: 343 us -> 0 us
  Pallas kernels: 0 us -> 187 us
  local copies, waits for them, and re-layouts: 97.2 us -> 7.32 us
  matrix products: 79.6 us -> 0 us
  blocking collectives: 49.8 us -> 0 us
  between operations: 13.8 us -> 0.67 us
  other arithmetic: 6.41 us -> 0.01 us
    pallas_call x0 -> x1, Pallas kernels: none -> 187 us  [body(): call(act_loc[0].transpose(1, 2, 0, 3), w_loc[0].reshape(9, 128, 1024), sc...]
    reduce_scatter x1 -> x0, waiting for transfers between devices: 174 us -> none  [body(): pre_out = lax.psum_scatter(part_sum, 'tp', scatter_dimension=3, tiled=True)]
    all_gather x1 -> x0, waiting for transfers between devices: 84.2 us -> none  [body(): grad_full = lax.all_gather(grad_blk, 'tp', axis=3, tiled=True)]
    conv_general_dilated x3 -> x0, matrix products: 79.6 us -> none  [the longest x1 33.1 us: conv_input_grad(): lax.conv_general_dilated(grad_out, kernel[::-1, ::-1], (1, 1), 'SAME', di...]
    ppermute x2 -> x0, waiting for transfers between devices: 72.1 us -> none  [the longest x1 37.5 us: body(): act_blk = lax.ppermute(moved, 'stage', perm=[(0, 1)])]
    unnamed x13 -> x9, local copies, waits for them, and re-layouts: 71.9 us -> 7.32 us
    all_to_all x2 -> x0, blocking collectives: 49.8 us -> none  [the longest x1 25.3 us: body(): dact_img = lax.all_to_all(dact_back, 'tp', 0, 3, tiled=True)]
    all_to_all x2 -> x0, local copies, waits for them, and re-layouts: 20.5 us -> none  [the longest x1 18.1 us: body(): moved = lax.all_to_all(images, 'tp', 3, 0, tiled=True)]
  transfers between devices with their start and end apart: 5 -> 0, of which waited for: 5 -> 0; matrix products, arithmetic and copies ran while one was open for 7% -> 0% of each run, Pallas kernels for 0% -> 0%
where the time goes in v2:
time: 198 us; the launch traced here: 195 us
  Pallas kernels  187 us (94%)
  local copies, waits for them, and re-layouts  7.32 us (4%)
    pallas_call x1, Pallas kernels, body(): call(act_loc[0].transpose(1, 2, 0, 3), w_loc[0].reshape(9, 128, 1024), sc...  187 us
    unnamed x9, local copies, waits for them, and re-layouts  7.32 us

profile of v2, /device:TPU:4, one launch (start us, length us, event | category | flops | bytes accessed | tf_op | source)
XLA Modules:
  0.0 195.1 jit_solution(18256885347957039728)
XLA Ops:
  0.6 187.1 %conv_block.1 = (bf16[28,28,8,256]{3,2,1,0:T(8,128)(2,1)}, bf16[28,28,2,512]{3,2,1,0:T(2,128)(2,1)}, f32[9,128,1024]{2,1,0:T(8,128)}) custom-call(bf16[28,28,2,512]{3,2,1,0:T(2,128)(2,1)} %bitcast.21, bf16[9,128,1024]{2,1,0:T(8,128)(2,1)} %bitcast.19, f32[1,256]{1,0:T(1,128)} %sc.1, f32[1,256]{1,0:T(1,128)} %sh.1, bf16[28,28,8,256]{3,2,1,0:T(8,128)(2,1)} %bitcast.18), custom_call_target="tpu_custom_call" | custom-call | tf_op jit(solution)/shard_map/conv_block/pallas_call | solution.py:308
  187.8 0.0 slice-start
  187.8 0.0 copy-start
  187.8 0.0 slice-start.1
  187.8 4.0 %copy.11 = bf16[1,8,28,28,256]{4,1,3,2,0:T(8,128)(2,1)} copy(bf16[1,8,28,28,256]{4,1,3,2,0:T(8,128)(2,1)} %bitcast.17) | data formatting | bytes 6422528
  191.8 0.0 copy-done
  191.8 1.2 copy.12
  192.9 0.0 slice-done
  192.9 0.0 slice-done.1
  192.9 2.2 %copy.13 = f32[1,3,3,128,1024]{4,3,2,1,0:T(8,128)} copy(f32[1,3,3,128,1024]{4,3,2,1,0:T(8,128)S(1)} %bitcast.16) | data formatting | bytes 9437184
  (1 shorter events, 0.0 us)
Async XLA Ops:
  187.8 5.2 %slice-start = ((s8[4718592]{0:T(1024)(128)(4,1)}), s8[4194304]{0:T(1024)(128)(4,1)S(1)}, s32[]{:S(2)}) async-start(s8[4718592]{0:T(1024)(128)(4,1)} %bitcast.14), calls=%async_computation | async-start | bytes 8388608
  187.8 4.0 %copy-start = (bf16[28,28,2,512]{3,2,1,0:T(2,128)(2,1)S(1)}, bf16[28,28,2,512]{3,2,1,0:T(2,128)(2,1)}, u32[]{:S(2)}) copy-start(bf16[28,28,2,512]{3,2,1,0:T(2,128)(2,1)} %get-tuple-element.7) | copy-start | bytes 4816900
  187.8 5.1 %slice-start.1 = ((s8[4718592]{0:T(1024)(128)(4,1)}), s8[524288]{0:T(1024)(128)(4,1)S(1)}, s32[]{:S(2)}) async-start(s8[4718592]{0:T(1024)(128)(4,1)} %bitcast.14), calls=%async_computation.1 | async-start | bytes 1048576

commit v3 on v2

--- a/solution.py
+++ b/solution.py
@@ -11,11 +11,13 @@
 F32 = jnp.float32
 MESH = pl.DeviceIdType.MESH
 CH = 4
-CR = 7
+CB = (0, 8, 15, 22, 28)
+GP = ((0, 15), (15, 13))
 
 
 def kernel(act, w, sc, sh, gz, z_out, da_out, dw_out, A, AC, KO, KCU, KT, DZ, GU, W, WR, ACC, DAO, ZB,
-           lsem, ksem_s, ksem_r, kc_s, kc_r, kc_l, as_s, a_r, f_s, g_s, g_r, zx_s, zx_r, da_s, da_r, out_s):
+           lsem, ksem_s, ksem_r, kc_s, kc_r, kc_l, as_s, ax_r, a_r, f_s, gs_s, gs_r, g2_s, g2_r, g3_s, g3_r, rel_s, rel_r,
+           zx_s, zx_r, d_s, d_r, da_s, da_r, out_s):
     dp = lax.axis_index("dp")
     stage = lax.axis_index("stage")
     t = lax.axis_index("tp")
@@ -24,6 +26,8 @@
     sib = x * 2 + (1 - k)
     xn = (1 - x) * 2 + k
     dg = (1 - x) * 2 + (1 - k)
+    pz = (1 - x) * 2 + (k + dp) % 2
+    pz2 = (1 - x) * 2 + (k + 1 - dp) % 2
     base = (1 - x) * 512
 
     def al(v, m):
@@ -54,19 +58,30 @@
     pl.semaphore_signal(barrier, inc=1, device_id={"dp": 1 - dp}, device_id_type=MESH)
     pl.semaphore_wait(barrier, 8)
 
+    def k_slot(src_tp):
+        return KO.at[:, pl.ds(al(128 * src_tp, 128), 128), :]
+
     def k_copy(rel, peer, src_tp):
-        return remote(w.at[:, :, pl.ds(al(256 * peer, 256), 256)], KO.at[:, pl.ds(al(128 * src_tp, 128), 128), :],
-                      ksem_s.at[rel], ksem_r.at[rel], tp=peer)
+        return remote(w.at[:, :, pl.ds(al(256 * peer, 256), 256)], k_slot(src_tp), ksem_s.at[rel], ksem_r.at[rel], tp=peer)
+
+    def k_z(src_tp):
+        return remote(k_slot(src_tp), k_slot(src_tp), ksem_s.at[2], ksem_r.at[2], dp=1 - dp)
 
     def kc_pieces(own, other):
         return ((0, 0, 256, 256 * own), (1, 0, 256, 256 * other), (2, 0, 128, base), (2, 128, 128, base + 256),
                 (3, 0, 128, base + 128), (3, 128, 128, base + 384))
 
     def a_slot(src, c):
-        return A.at[pl.ds(1 + CR * c, CR), pl.ds(1, 28), pl.ds(2 * src, 2), :]
+        return A.at[pl.ds(1 + CB[c], CB[c + 1] - CB[c]), pl.ds(1, 28), pl.ds(2 * src, 2), :]
 
     def a_direct(c):
-        return remote(act.at[pl.ds(CR * c, CR)], a_slot(t, c), as_s.at[c], a_r.at[3, c], stage=1)
+        return remote(act.at[pl.ds(CB[c], CB[c + 1] - CB[c])], a_slot(t, c), as_s.at[c], a_r.at[3, c], stage=1)
+
+    def a_cross():
+        return remote(act.at[pl.ds(CB[3], CB[4] - CB[3])], a_slot(t, 3), as_s.at[4], ax_r.at[0], tp=xn)
+
+    def a_cross_fwd():
+        return remote(a_slot(xn, 3), a_slot(xn, 3), as_s.at[5], a_r.at[1, 3], stage=1)
 
     def a_fwd(kind, c):
         if kind == 0:
@@ -78,8 +93,28 @@
     def a_recv(rel, src, c):
         return remote(a_slot(src, c), a_slot(src, c), f_s.at[0, c], a_r.at[rel, c], tp=sib)
 
-    def g_inner(u, lane, width):
-        return GU.at[u, pl.ds(1, 28), pl.ds(1, 28), :, pl.ds(lane, width)]
+    def g_rows(u, r0, n, lane, width):
+        return GU.at[u, pl.ds(1 + r0, n), pl.ds(1, 28), :, pl.ds(lane, width)]
+
+    mine = al(128 * k, 128)
+    theirs = al(128 * (1 - k), 128)
+
+    def g2(c):
+        return remote(g_rows(0, 7 * c, 7, 0, 128), g_rows(2, 7 * c, 7, mine, 128), g2_s.at[c], g2_r.at[c], tp=xn)
+
+    def g3(p):
+        return remote(g_rows(0, GP[p][0], GP[p][1], 128, 128), g_rows(3, GP[p][0], GP[p][1], mine, 128), g3_s.at[p], g3_r.at[p], tp=xn)
+
+    def g2_rel(lane):
+        return remote(g_rows(2, 0, 28, lane, 128), g_rows(2, 0, 28, lane, 128), rel_s.at[0], rel_r.at[0], tp=sib)
+
+    def g3_rel(p, lane):
+        return remote(g_rows(3, GP[p][0], GP[p][1], lane, 128), g_rows(3, GP[p][0], GP[p][1], lane, 128), rel_s.at[1 + p], rel_r.at[1 + p], tp=sib)
+
+    def det(leg, p):
+        src, dst = ((W, WR), (WR, W), (W, WR))[leg]
+        dev = ({"stage": 0}, {"dp": 1 - dp}, {"stage": 1})[leg]
+        return remote(src.at[1, pl.ds(3 * p, 3)], dst.at[1, pl.ds(3 * p, 3)], d_s.at[leg, p], d_r.at[leg, p], **dev)
 
     def da_copy(s, n):
         return remote(DAO.at[pl.ds(2 * n, 2), :, pl.ds(2 * s, 2), :],
@@ -88,8 +123,11 @@
 
     @pl.when(stage == 0)
     def _():
+        a_cross().start()
         for c in range(CH):
             a_direct(c).start()
+        a_cross().wait_recv()
+        a_cross_fwd().start()
         W[0] = jnp.zeros((9, 128, 256), F32)
 
         def zrow(h, carry):
@@ -103,8 +141,16 @@
             o.start()
         for o in outs:
             o.wait()
+        for leg, p in ((0, 0), (0, 1), (1, 0), (0, 2), (1, 1), (1, 2)):
+            det(leg, p).wait_recv()
+            det(leg + 1, p).start()
         for c in range(CH):
             a_direct(c).wait_send()
+        a_cross().wait_send()
+        a_cross_fwd().wait_send()
+        for p in range(3):
+            det(1, p).wait_send()
+            det(2, p).wait_send()
         for src in range(4):
             for n in range(7):
                 remote(DAO.at[pl.ds(2 * n, 2), :, pl.ds(0, 2), :],
@@ -113,8 +159,7 @@
 
     @pl.when(stage == 1)
     def _():
-        k_copy(1, xn, t).start()
-        k_copy(2, dg, t).start()
+        k_copy(1, pz, t).start()
         k_copy(0, sib, t).start()
         for i, (u, lane, wd, src) in enumerate(kc_pieces(sib, t)):
             remote(w.at[:, :, pl.ds(al(src, 128), wd)], KCU.at[u, :, pl.ds(al(128 * k, 128), 128), pl.ds(lane, wd)],
@@ -133,7 +178,8 @@
 
         for c in range(CH):
             a_recv(3, t, c).wait_recv()
-            a_fwd(1, c).start()
+            if c < 3:
+                a_fwd(1, c).start()
             a_fwd(0, c).start()
             if c == 0:
                 for o in loc:
@@ -143,6 +189,9 @@
                 for i, (u, lane, wd, src) in enumerate(kc_pieces(t, sib)):
                     remote(w.at[:, :, pl.ds(al(src, 128), wd)], KCU.at[u, :, pl.ds(al(128 * (1 - k), 128), 128), pl.ds(lane, wd)],
                            kc_s.at[i], kc_r.at[i], tp=sib).wait_recv()
+            if c == 1:
+                k_copy(1, t, pz).wait_recv()
+                k_z(pz).start()
 
             def tr(tap, carry, c=c):
                 KT[c, pl.ds(tap * 256, 256)] = KCU[c, tap].T
@@ -150,44 +199,39 @@
 
             lax.fori_loop(0, 9, tr, 0)
 
-        k_copy(1, t, xn).wait_recv()
-        k_copy(2, t, dg).wait_recv()
+        k_z(pz2).wait_recv()
         k_copy(0, t, sib).wait_recv()
 
-        def chunk(c, carry):
+        def row(h, carry):
+            lhs = jnp.concatenate([A[h + i, j:j + 28].reshape(224, 512) for i in range(3) for j in range(3)], axis=1)
+            pre = jnp.dot(lhs, KO[...].reshape(4608, 256), preferred_element_type=F32)
+            y = pre * sc[...] + sh[...]
+            d = DZ[h].reshape(224, 256).astype(F32)
+            g = jnp.where(y > 0, d * sc[...], 0.0).astype(BF)
+            DZ[h] = jnp.maximum(y, 0.0).astype(BF).reshape(28, 8, 256)
+            GU[0, h + 1, 1:29] = g.reshape(28, 8, 256)
+            return carry
+
+        z_cp = pltpu.make_async_copy(DZ, z_out, lsem.at[0])
+        ac_cp = pltpu.make_async_copy(A.at[:, :, :, pl.ds(al(128 * t, 128), 128)], AC, lsem.at[1])
+        g_sib = remote(GU.at[0], GU.at[1], gs_s.at[0], gs_r.at[0], tp=sib)
+
+        for c in range(CH):
             a_recv(1, xn, c).wait_recv()
             a_fwd(2, c).start()
             a_recv(0, sib, c).wait_recv()
             a_recv(2, dg, c).wait_recv()
-
-            def row(h, inner):
-                lhs = jnp.concatenate([A[h + i, j:j + 28].reshape(224, 512) for i in range(3) for j in range(3)], axis=1)
-                pre = jnp.dot(lhs, KO[...].reshape(4608, 256), preferred_element_type=F32)
-                y = pre * sc[...] + sh[...]
-                d = DZ[h].reshape(224, 256).astype(F32)
-                g = jnp.where(y > 0, d * sc[...], 0.0).astype(BF)
-                DZ[h] = jnp.maximum(y, 0.0).astype(BF).reshape(28, 8, 256)
-                GU[0, h + 1, 1:29] = g.reshape(28, 8, 256)
-                return inner
-
-            lax.fori_loop(CR * c - (c + 2) // 3, CR * (c + 1) - 1 + c // 3, row, 0)
-            return carry
-
-        lax.fori_loop(0, CH, chunk, 0)
-
-        z_cp = pltpu.make_async_copy(DZ, z_out, lsem.at[0])
-        ac_cp = pltpu.make_async_copy(A.at[:, :, :, pl.ds(al(128 * t, 128), 128)], AC, lsem.at[1])
-        g_sib = remote(GU.at[0], GU.at[1], g_s.at[0], g_r.at[0], tp=sib)
-        g_x = [remote(g_inner(0, 128 * q, 128), g_inner(2 + q, al(128 * k, 128), 128), g_s.at[1 + q], g_r.at[1 + q], tp=xn) for q in range(2)]
-        g_rel = [remote(g_inner(2 + q, al(128 * k, 128), 128), g_inner(2 + q, al(128 * k, 128), 128), g_s.at[3 + q], g_r.at[3 + q], tp=sib) for q in range(2)]
-        ac_cp.start()
-        g_x[0].start()
-        g_x[1].start()
+            if c == CH - 1:
+                ac_cp.start()
+            lax.fori_loop(7 * c, 7 * c + 7, row, 0)
+            g2(c).start()
+        for p in range(2):
+            g3(p).start()
         g_sib.start()
         z_cp.start()
         ac_cp.wait()
 
-        zx = [remote(W.at[u], WR.at[u], zx_s.at[u], zx_r.at[u], dp=1 - dp) for u in range(4)]
+        zx = {u: remote(W.at[u], WR.at[u], zx_s.at[u], zx_r.at[u], dp=1 - dp) for u in (0, 2, 3)}
 
         def dw_unit(u):
             W[u] = jnp.zeros((9, 128, 256), F32)
@@ -201,7 +245,11 @@
                 return carry
 
             lax.fori_loop(0, 4, step, 0)
-            zx[u].start()
+            if u == 1:
+                for p in range(3):
+                    det(0, p).start()
+            else:
+                zx[u].start()
 
         def da_rows(u, n):
             h = 14 * k + 2 * n
@@ -224,7 +272,11 @@
                     for i, s in enumerate(starts)]
 
         def dw_final(u):
-            zx[u].wait_recv()
+            if u == 1:
+                for p in range(3):
+                    det(2, p).wait_recv()
+            else:
+                zx[u].wait_recv()
 
             def add(q, carry):
                 WR[u, q] += W[u, q]
@@ -239,16 +291,6 @@
         dw_unit(1)
         da_unit(0)
         da_unit(1)
-        for q in range(2):
-            u = 2 + q
-            g_x[q].wait_recv()
-            g_rel[q].start()
-            remote(g_inner(u, 0, 128), g_inner(u, al(128 * (1 - k), 128), 128), g_s.at[3 + q], g_r.at[3 + q], tp=sib).wait_recv()
-            dw_unit(u)
-            if q == 0:
-                da_unit(2)
-                dw_final(0)
-
         def last(n, carry):
             v = ACC[pl.ds(2 * n, 2)].reshape(448, 256) + da_rows(3, n)
             DAO[pl.ds(2 * n, 2)] = v.astype(BF).reshape(2, 28, 8, 256)
@@ -256,28 +298,58 @@
                 da_copy(s, n).start()
             return carry
 
-        lax.fori_loop(0, 7, last, 0)
-        for u in range(1, 4):
+        for c in range(CH):
+            g2(c).wait_recv()
+        g2_rel(mine).start()
+        g2_rel(theirs).wait_recv()
+        dw_unit(2)
+        da_unit(2)
+        dw_final(0)
+        g3(0).wait_recv()
+        g3_rel(0, mine).start()
+        g3_rel(0, theirs).wait_recv()
+
+        @pl.when(k == 0)
+        def _():
+            lax.fori_loop(0, 7, last, 0)
+
+        dw_final(1)
+        g3(1).wait_recv()
+        g3_rel(1, mine).start()
+        g3_rel(1, theirs).wait_recv()
+        dw_unit(3)
+
+        @pl.when(k == 1)
+        def _():
+            lax.fori_loop(0, 7, last, 0)
+
+        for u in range(2, 4):
             dw_final(u)
 
         z_cp.wait()
         for u in range(4):
             for o in dw_out_cp(u):
                 o.wait()
-            zx[u].wait_send()
-        k_copy(1, xn, t).wait_send()
-        k_copy(2, dg, t).wait_send()
+            if u != 1:
+                zx[u].wait_send()
+        for p in range(3):
+            det(0, p).wait_send()
+        k_copy(1, pz, t).wait_send()
+        k_z(pz).wait_send()
         k_copy(0, sib, t).wait_send()
         for i, (u, lane, wd, src) in enumerate(kc_pieces(sib, t)):
             remote(w.at[:, :, pl.ds(al(src, 128), wd)], KCU.at[u, :, pl.ds(al(128 * k, 128), 128), pl.ds(lane, wd)],
                    kc_s.at[i], kc_r.at[i], tp=sib).wait_send()
         for c in range(CH):
             for kind in range(3):
-                a_fwd(kind, c).wait_send()
+                if kind != 1 or c < 3:
+                    a_fwd(kind, c).wait_send()
+            g2(c).wait_send()
         g_sib.wait_send()
-        for q in range(2):
-            g_x[q].wait_send()
-            g_rel[q].wait_send()
+        g2_rel(mine).wait_send()
+        for p in range(2):
+            g3(p).wait_send()
+            g3_rel(p, mine).wait_send()
         for s in range(4):
             for n in range(7):
                 da_copy(s, n).wait_send()
@@ -297,8 +369,8 @@
             V((30, 30, 8, 512), BF), V((30, 30, 8, 128), BF), V((9, 512, 256), BF), V((4, 9, 256, 256), BF), V((4, 2304, 256), BF),
             V((28, 28, 8, 256), BF), V((4, 30, 30, 8, 256), BF), V((4, 9, 128, 256), F32), V((4, 9, 128, 256), F32),
             V((14, 224, 256), F32), V((14, 28, 8, 256), BF), V((7, 28, 2, 512), BF),
-            D((2,)), D((3,)), D((3,)), D((6,)), D((6,)), D((6,)), D((4,)), D((4, 4)), D((3, 4)), D((5,)), D((5,)), D((4,)), D((4,)),
-            D((4, 7)), D((4, 7)), D((5,)),
+            D((2,)), D((3,)), D((3,)), D((6,)), D((6,)), D((6,)), D((6,)), D((1,)), D((4, 4)), D((3, 4)), D((1,)), D((1,)), D((4,)), D((4,)),
+            D((2,)), D((2,)), D((3,)), D((3,)), D((4,)), D((4,)), D((3, 3)), D((3, 3)), D((4, 7)), D((4, 7)), D((5,)),
         ],
         compiler_params=pltpu.CompilerParams(collective_id=0, has_side_effects=True, vmem_limit_bytes=66000000),
         name="conv_block",

time: 198 us -> 172 us (0.87)
  Pallas kernels: 187 us -> 163 us
    pallas_call x1, Pallas kernels: 187 us -> 163 us  [body(): call(act_loc[0].transpose(1, 2, 0, 3), w_loc[0].reshape(9, 128, 1024), sc...]
where the time goes in v3:
time: 172 us; the launch traced here: 171 us
  Pallas kernels  163 us (95%)
  local copies, waits for them, and re-layouts  7.32 us (4%)
    pallas_call x1, Pallas kernels, body(): call(act_loc[0].transpose(1, 2, 0, 3), w_loc[0].reshape(9, 128, 1024), sc...  163 us
    unnamed x9, local copies, waits for them, and re-layouts  7.32 us

profile of v3, /device:TPU:4, one launch (start us, length us, event | category | flops | bytes accessed | tf_op | source)
XLA Modules:
  0.0 171.1 jit_solution(1158112760253029949)
XLA Ops:
  0.6 163.1 %conv_block.1 = (bf16[28,28,8,256]{3,2,1,0:T(8,128)(2,1)}, bf16[28,28,2,512]{3,2,1,0:T(2,128)(2,1)}, f32[9,128,1024]{2,1,0:T(8,128)}) custom-call(bf16[28,28,2,512]{3,2,1,0:T(2,128)(2,1)} %bitcast.21, bf16[9,128,1024]{2,1,0:T(8,128)(2,1)} %bitcast.19, f32[1,256]{1,0:T(1,128)} %sc.1, f32[1,256]{1,0:T(1,128)} %sh.1, bf16[28,28,8,256]{3,2,1,0:T(8,128)(2,1)} %bitcast.18), custom_call_target="tpu_custom_call" | custom-call | tf_op jit(solution)/shard_map/conv_block/pallas_call | solution.py:380
  163.7 0.0 slice-start
  163.7 0.0 copy-start
  163.8 0.0 slice-start.1
  163.8 4.0 %copy.11 = bf16[1,8,28,28,256]{4,1,3,2,0:T(8,128)(2,1)} copy(bf16[1,8,28,28,256]{4,1,3,2,0:T(8,128)(2,1)} %bitcast.17) | data formatting | bytes 6422528
  167.7 0.0 copy-done
  167.7 1.2 copy.12
  168.9 0.0 slice-done
  168.9 0.0 slice-done.1
  168.9 2.2 %copy.13 = f32[1,3,3,128,1024]{4,3,2,1,0:T(8,128)} copy(f32[1,3,3,128,1024]{4,3,2,1,0:T(8,128)S(1)} %bitcast.16) | data formatting | bytes 9437184
  (1 shorter events, 0.0 us)
Async XLA Ops:
  163.7 5.2 %slice-start = ((s8[4718592]{0:T(1024)(128)(4,1)}), s8[4194304]{0:T(1024)(128)(4,1)S(1)}, s32[]{:S(2)}) async-start(s8[4718592]{0:T(1024)(128)(4,1)} %bitcast.14), calls=%async_computation | async-start | bytes 8388608
  163.7 4.0 %copy-start = (bf16[28,28,2,512]{3,2,1,0:T(2,128)(2,1)S(1)}, bf16[28,28,2,512]{3,2,1,0:T(2,128)(2,1)}, u32[]{:S(2)}) copy-start(bf16[28,28,2,512]{3,2,1,0:T(2,128)(2,1)} %get-tuple-element.7) | copy-start | bytes 4816900
  163.8 5.1 %slice-start.1 = ((s8[4718592]{0:T(1024)(128)(4,1)}), s8[524288]{0:T(1024)(128)(4,1)S(1)}, s32[]{:S(2)}) async-start(s8[4718592]{0:T(1024)(128)(4,1)} %bitcast.14), calls=%async_computation.1 | async-start | bytes 1048576

commit v4 on v3

v4 whole, which is shorter than its diff:
```python
import functools

import jax
import jax.numpy as jnp
from jax import lax
from jax.experimental import pallas as pl
from jax.experimental.pallas import tpu as pltpu
from jax.sharding import PartitionSpec as P

BF = jnp.bfloat16
F32 = jnp.float32
MESH = pl.DeviceIdType.MESH
CH = 4
CB = (0, 8, 15, 22, 28)
GP = ((0, 8), (8, 7), (20, 8), (15, 5))
HW = 28
HP = 30
NB = 8
RW = 224
TAPS = 9
LN = 128
BLK = 256
CIN = 512


def kernel(act, w, sc, sh, gz, z_out, da_out, dw_out, A, AC, KO, KCU, KT, DZ, GU, W, WR, ACC, DAO, ZB,
           lsem, ksem_s, ksem_r, kc_s, kc_r, kc_l, as_s, ax_r, a_r, f_s, gs_s, gs_r, g2_s, g2_r, g3_s, g3_r, gd_s, gd_r, rel_s, rel_r,
           zx_s, zx_r, d_s, d_r, da_s, da_r, out_s):
    dp = lax.axis_index("dp")
    stage = lax.axis_index("stage")
    t = lax.axis_index("tp")
    x = t // 2
    k = t % 2
    sib = x * 2 + (1 - k)
    xn = (1 - x) * 2 + k
    dg = (1 - x) * 2 + (1 - k)
    pz = (1 - x) * 2 + (k + dp) % 2
    pz2 = (1 - x) * 2 + (k + 1 - dp) % 2
    base = (1 - x) * CIN

    def al(v, m):
        return pl.multiple_of(v, m)

    def remote(src, dst, ssem, rsem, **dev):
        return pltpu.make_async_remote_copy(src_ref=src, dst_ref=dst, send_sem=ssem, recv_sem=rsem, device_id=dev, device_id_type=MESH)

    A[0] = jnp.zeros((HP, NB, CIN), BF)
    A[29] = jnp.zeros((HP, NB, CIN), BF)
    A[:, 0] = jnp.zeros((HP, NB, CIN), BF)
    A[:, 29] = jnp.zeros((HP, NB, CIN), BF)

    def zero_halo(u, carry):
        GU[u, 0] = jnp.zeros((HP, NB, BLK), BF)
        GU[u, 29] = jnp.zeros((HP, NB, BLK), BF)
        GU[u, :, 0] = jnp.zeros((HP, NB, BLK), BF)
        GU[u, :, 29] = jnp.zeros((HP, NB, BLK), BF)
        return carry

    lax.fori_loop(0, 4, zero_halo, 0)

    barrier = pltpu.get_barrier_semaphore()
    for ds in range(2):
        for dt in range(4):
            if ds or dt:
                pl.semaphore_signal(barrier, inc=1, device_id={"stage": (stage + ds) % 2, "tp": (t + dt) % 4}, device_id_type=MESH)
    pl.semaphore_signal(barrier, inc=1, device_id={"dp": 1 - dp}, device_id_type=MESH)
    pl.semaphore_wait(barrier, NB)

    def k_slot(src_tp):
        return KO.at[:, pl.ds(al(LN * src_tp, LN), LN), :]

    def k_copy(rel, peer, src_tp):
        return remote(w.at[:, :, pl.ds(al(BLK * peer, BLK), BLK)], k_slot(src_tp), ksem_s.at[rel], ksem_r.at[rel], tp=peer)

    def k_z(src_tp):
        return remote(k_slot(src_tp), k_slot(src_tp), ksem_s.at[2], ksem_r.at[2], dp=1 - dp)

    def kc_pieces(own, other):
        return ((0, 0, BLK, BLK * own), (1, 0, BLK, BLK * other), (2, 0, LN, base), (2, LN, LN, base + BLK),
                (3, 0, LN, base + LN), (3, LN, LN, base + 384))

    def a_slot(src, c):
        return A.at[pl.ds(1 + CB[c], CB[c + 1] - CB[c]), pl.ds(1, HW), pl.ds(2 * src, 2), :]

    def a_direct(c):
        return remote(act.at[pl.ds(CB[c], CB[c + 1] - CB[c])], a_slot(t, c), as_s.at[c], a_r.at[3, c], stage=1)

    def a_cross():
        return remote(act.at[pl.ds(CB[3], CB[4] - CB[3])], a_slot(t, 3), as_s.at[4], ax_r.at[0], tp=xn)

    def a_cross_fwd():
        return remote(a_slot(xn, 3), a_slot(xn, 3), as_s.at[5], a_r.at[1, 3], stage=1)

    def a_fwd(kind, c):
        if kind == 0:
            return remote(a_slot(t, c), a_slot(t, c), f_s.at[0, c], a_r.at[0, c], tp=sib)
        if kind == 1:
            return remote(a_slot(t, c), a_slot(t, c), f_s.at[1, c], a_r.at[1, c], tp=xn)
        return remote(a_slot(xn, c), a_slot(xn, c), f_s.at[2, c], a_r.at[2, c], tp=sib)

    def a_recv(rel, src, c):
        return remote(a_slot(src, c), a_slot(src, c), f_s.at[0, c], a_r.at[rel, c], tp=sib)

    def g_rows(u, r0, n, lane, width):
        return GU.at[u, pl.ds(1 + r0, n), pl.ds(1, HW), :, pl.ds(lane, width)]

    mine = al(LN * k, LN)
    theirs = al(LN * (1 - k), LN)

    def g2(c):
        return remote(g_rows(0, 7 * c, 7, 0, LN), g_rows(2, 7 * c, 7, mine, LN), g2_s.at[c], g2_r.at[c], tp=xn)

    def g3(p):
        return remote(g_rows(0, GP[p][0], GP[p][1], LN, LN), g_rows(3, GP[p][0], GP[p][1], mine, LN), g3_s.at[p], g3_r.at[p], tp=xn)

    def g2_rel(lane):
        return remote(g_rows(2, 0, HW, lane, LN), g_rows(2, 0, HW, lane, LN), rel_s.at[0], rel_r.at[0], tp=sib)

    def g3_rel(p, lane):
        return remote(g_rows(3, GP[p][0], GP[p][1], lane, LN), g_rows(3, GP[p][0], GP[p][1], lane, LN), rel_s.at[1 + p], rel_r.at[1 + p], tp=sib)

    def gdet(leg, p):
        r0, n = GP[p]
        own = g_rows(0, r0, n, LN, LN)
        a3 = g_rows(3, r0, n, mine, LN)
        a2 = g_rows(2, r0, n, mine, LN)
        src, dst, dev = ((own, a3, {"stage": 0}), (a3, a2, {"tp": xn}), (a2, a3, {"stage": 1}))[leg]
        return remote(src, dst, gd_s.at[leg, p - 2], gd_r.at[leg, p - 2], **dev)

    def det(leg, p):
        src, dst = ((W, WR), (WR, W), (W, WR))[leg]
        dev = ({"stage": 0}, {"dp": 1 - dp}, {"stage": 1})[leg]
        return remote(src.at[1, pl.ds(3 * p, 3)], dst.at[1, pl.ds(3 * p, 3)], d_s.at[leg, p], d_r.at[leg, p], **dev)

    def da_copy(s, n):
        return remote(DAO.at[pl.ds(2 * n, 2), :, pl.ds(2 * s, 2), :],
                      da_out.at[pl.ds(14 * k + 2 * n, 2), :, :, pl.ds(al(BLK * x, BLK), BLK)],
                      da_s.at[s, n], da_r.at[t, n], stage=0, tp=s)

    @pl.when(stage == 0)
    def _():
        a_cross().start()
        for c in range(CH):
            a_direct(c).start()
        a_cross().wait_recv()
        a_cross_fwd().start()
        W[0] = jnp.zeros((TAPS, LN, BLK), F32)

        def zrow(h, carry):
            DZ[h] = jnp.zeros((HW, NB, BLK), BF)
            return carry

        lax.fori_loop(0, HW, zrow, 0)
        outs = [pltpu.make_async_copy(W.at[0], dw_out.at[:, :, pl.ds(BLK * u, BLK)], out_s.at[u]) for u in range(4)]
        outs.append(pltpu.make_async_copy(DZ, z_out, out_s.at[4]))
        for o in outs:
            o.start()
        for o in outs:
            o.wait()
        for leg in range(2):
            for p in (2, 3):
                gdet(leg, p).wait_recv()
                gdet(leg + 1, p).start()
        for leg, p in ((0, 0), (0, 1), (1, 0), (0, 2), (1, 1), (1, 2)):
            det(leg, p).wait_recv()
            det(leg + 1, p).start()
        for c in range(CH):
            a_direct(c).wait_send()
        a_cross().wait_send()
        a_cross_fwd().wait_send()
        for p in range(3):
            det(1, p).wait_send()
            det(2, p).wait_send()
        for p in (2, 3):
            gdet(1, p).wait_send()
            gdet(2, p).wait_send()
        for src in range(4):
            for n in range(7):
                remote(DAO.at[pl.ds(2 * n, 2), :, pl.ds(0, 2), :],
                       da_out.at[pl.ds(14 * (src % 2) + 2 * n, 2), :, :, pl.ds(BLK * (src // 2), BLK)],
                       da_s.at[0, n], da_r.at[src, n], stage=0, tp=0).wait_recv()

    @pl.when(stage == 1)
    def _():
        k_copy(1, pz, t).start()
        k_copy(0, sib, t).start()
        for i, (u, lane, wd, src) in enumerate(kc_pieces(sib, t)):
            remote(w.at[:, :, pl.ds(al(src, LN), wd)], KCU.at[u, :, pl.ds(al(LN * k, LN), LN), pl.ds(lane, wd)],
                   kc_s.at[i], kc_r.at[i], tp=sib).start()
        loc = [pltpu.make_async_copy(w.at[:, :, pl.ds(al(src, LN), wd)], KCU.at[u, :, pl.ds(al(LN * k, LN), LN), pl.ds(lane, wd)], kc_l.at[i])
               for i, (u, lane, wd, src) in enumerate(kc_pieces(t, sib))]
        loc.append(pltpu.make_async_copy(w.at[:, :, pl.ds(al(BLK * t, BLK), BLK)], KO.at[:, pl.ds(al(LN * t, LN), LN), :], lsem.at[0]))
        loc.append(pltpu.make_async_copy(gz, DZ, lsem.at[1]))
        for o in loc:
            o.start()
        ZB[...] = jnp.zeros((7, HW, 2, CIN), BF)
        zcp = [pltpu.make_async_copy(ZB, da_out.at[pl.ds(7 * i, 7)], out_s.at[i]) for i in range(4)]
        for o in zcp:
            o.start()
        ACC[...] = jnp.zeros((14, RW, BLK), F32)

        for c in range(CH):
            a_recv(3, t, c).wait_recv()
            if c < 3:
                a_fwd(1, c).start()
            a_fwd(0, c).start()
            if c == 0:
                for o in loc:
                    o.wait()
                for o in zcp:
                    o.wait()
                for i, (u, lane, wd, src) in enumerate(kc_pieces(t, sib)):
                    remote(w.at[:, :, pl.ds(al(src, LN), wd)], KCU.at[u, :, pl.ds(al(LN * (1 - k), LN), LN), pl.ds(lane, wd)],
                           kc_s.at[i], kc_r.at[i], tp=sib).wait_recv()
            if c == 1:
                k_copy(1, t, pz).wait_recv()
                k_z(pz).start()

            def tr(tap, carry, c=c):
                KT[c, pl.ds(tap * BLK, BLK)] = KCU[c, tap].T
                return carry

            lax.fori_loop(0, TAPS, tr, 0)

        k_z(pz2).wait_recv()
        k_copy(0, t, sib).wait_recv()

        def row(h, carry):
            lhs = jnp.concatenate([A[h + i, j:j + HW].reshape(RW, CIN) for i in range(3) for j in range(3)], axis=1)
            pre = jnp.dot(lhs, KO[...].reshape(4608, BLK), preferred_element_type=F32)
            y = pre * sc[...] + sh[...]
            d = DZ[h].reshape(RW, BLK).astype(F32)
            g = jnp.where(y > 0, d * sc[...], 0.0).astype(BF)
            DZ[h] = jnp.maximum(y, 0.0).astype(BF).reshape(HW, NB, BLK)
            GU[0, h + 1, 1:29] = g.reshape(HW, NB, BLK)
            return carry

        z_cp = pltpu.make_async_copy(DZ, z_out, lsem.at[0])
        ac_cp = pltpu.make_async_copy(A.at[:, :, :, pl.ds(al(LN * t, LN), LN)], AC, lsem.at[1])
        g_sib = remote(GU.at[0], GU.at[1], gs_s.at[0], gs_r.at[0], tp=sib)

        for c in range(CH):
            a_recv(1, xn, c).wait_recv()
            a_fwd(2, c).start()
            a_recv(0, sib, c).wait_recv()
            a_recv(2, dg, c).wait_recv()
            if c == CH - 1:
                ac_cp.start()
            lax.fori_loop(7 * c, 7 * c + 7, row, 0)
            g2(c).start()
        for p in (2, 3):
            gdet(0, p).start()
        g_sib.start()
        z_cp.start()
        ac_cp.wait()

        zx = {u: remote(W.at[u], WR.at[u], zx_s.at[u], zx_r.at[u], dp=1 - dp) for u in (0, 2, 3)}

        def dw_unit(u):
            W[u] = jnp.zeros((TAPS, LN, BLK), F32)

            def step(n, carry):
                h = n * 7
                lhs = jnp.concatenate([AC[pl.ds(h + i, 7), j:j + HW].reshape(1568, LN) for i in range(3) for j in range(3)], axis=1)
                rhs = GU[u, pl.ds(h + 1, 7), 1:29].reshape(1568, BLK)
                p = lax.dot_general(lhs, rhs, (((0,), (0,)), ((), ())), preferred_element_type=F32)
                W[u] += p.reshape(TAPS, LN, BLK)
                return carry

            lax.fori_loop(0, 4, step, 0)
            if u == 1:
                for p in range(3):
                    det(0, p).start()
            else:
                zx[u].start()

        def da_rows(u, n):
            h = 14 * k + 2 * n
            lhs = jnp.concatenate([GU[u, pl.ds(h + 2 - i, 2), 2 - j:HP - j].reshape(448, BLK) for i in range(3) for j in range(3)], axis=1)
            return jnp.dot(lhs, KT[u], preferred_element_type=F32)

        def da_unit(u):
            def step(n, carry):
                ACC[pl.ds(2 * n, 2)] += da_rows(u, n).reshape(2, RW, BLK)
                return carry

            lax.fori_loop(0, 7, step, 0)

        dw_dst = ((BLK * t,), (BLK * sib,), (base, base + BLK), (base + LN, base + 384))

        def dw_out_cp(u):
            starts = dw_dst[u]
            wd = BLK // len(starts)
            return [pltpu.make_async_copy(WR.at[u, :, :, pl.ds(wd * i, wd)], dw_out.at[:, :, pl.ds(al(s, LN), wd)], kc_l.at[2 * (u // 2) + (u % 2) * (u // 2) + u % 2 + i])
                    for i, s in enumerate(starts)]

        def dw_final(u):
            if u == 1:
                for p in range(3):
                    det(2, p).wait_recv()
            else:
                zx[u].wait_recv()

            def add(q, carry):
                WR[u, q] += W[u, q]
                return carry

            lax.fori_loop(0, TAPS, add, 0)
            for o in dw_out_cp(u):
                o.start()

        dw_unit(0)
        g_sib.wait_recv()
        dw_unit(1)
        da_unit(0)
        da_unit(1)
        def last(n, carry):
            v = ACC[pl.ds(2 * n, 2)].reshape(448, BLK) + da_rows(3, n)
            DAO[pl.ds(2 * n, 2)] = v.astype(BF).reshape(2, HW, NB, BLK)
            for s in range(4):
                da_copy(s, n).start()
            return carry

        def g3_arrive(p):
            if p < 2:
                g3(p).wait_recv()
            else:
                gdet(2, p).wait_recv()
            g3_rel(p, mine).start()
            g3_rel(p, theirs).wait_recv()

        for c in range(CH):
            g2(c).wait_send()
        g3(0).start()
        for c in range(CH):
            g2(c).wait_recv()
        g2_rel(mine).start()
        g2_rel(theirs).wait_recv()
        dw_unit(2)
        g3(0).wait_send()
        g3(1).start()
        da_unit(2)
        g3_arrive(2)

        @pl.when(k == 1)
        def _():
            lax.fori_loop(4, 7, last, 0)

        g3_arrive(0)

        @pl.when(k == 0)
        def _():
            lax.fori_loop(0, 3, last, 0)

        dw_final(0)
        g3_arrive(3)
        g3_arrive(1)
        dw_unit(3)
        lax.fori_loop(3 - 3 * k, 7 - 3 * k, last, 0)
        dw_final(1)
        for u in range(2, 4):
            dw_final(u)

        z_cp.wait()
        for u in range(4):
            for o in dw_out_cp(u):
                o.wait()
            if u != 1:
                zx[u].wait_send()
        for p in range(3):
            det(0, p).wait_send()
        k_copy(1, pz, t).wait_send()
        k_z(pz).wait_send()
        k_copy(0, sib, t).wait_send()
        for i, (u, lane, wd, src) in enumerate(kc_pieces(sib, t)):
            remote(w.at[:, :, pl.ds(al(src, LN), wd)], KCU.at[u, :, pl.ds(al(LN * k, LN), LN), pl.ds(lane, wd)],
                   kc_s.at[i], kc_r.at[i], tp=sib).wait_send()
        for c in range(CH):
            for kind in range(3):
                if kind != 1 or c < 3:
                    a_fwd(kind, c).wait_send()
        g_sib.wait_send()
        g2_rel(mine).wait_send()
        g3(1).wait_send()
        for p in (2, 3):
            gdet(0, p).wait_send()
        for p in range(4):
            g3_rel(p, mine).wait_send()
        for s in range(4):
            for n in range(7):
                da_copy(s, n).wait_send()


def solution(mesh):
    V = pltpu.VMEM
    D = pltpu.SemaphoreType.DMA
    any_spec = pl.BlockSpec(memory_space=pl.ANY)
    vm_spec = pl.BlockSpec(memory_space=pltpu.VMEM)
    call = pl.pallas_call(
        kernel,
        out_shape=[jax.ShapeDtypeStruct((HW, HW, NB, BLK), BF), jax.ShapeDtypeStruct((HW, HW, 2, CIN), BF), jax.ShapeDtypeStruct((TAPS, LN, 1024), F32)],
        in_specs=[any_spec, any_spec, vm_spec, vm_spec, any_spec],
        out_specs=[any_spec] * 3,
        scratch_shapes=[
            V((HP, HP, NB, CIN), BF), V((HP, HP, NB, LN), BF), V((TAPS, CIN, BLK), BF), V((4, TAPS, BLK, BLK), BF), V((4, 2304, BLK), BF),
            V((HW, HW, NB, BLK), BF), V((4, HP, HP, NB, BLK), BF), V((4, TAPS, LN, BLK), F32), V((4, TAPS, LN, BLK), F32),
            V((14, RW, BLK), F32), V((14, HW, NB, BLK), BF), V((7, HW, 2, CIN), BF),
            D((2,)), D((3,)), D((3,)), D((6,)), D((6,)), D((6,)), D((6,)), D((1,)), D((4, 4)), D((3, 4)), D((1,)), D((1,)), D((4,)), D((4,)),
            D((2,)), D((2,)), D((3, 2)), D((3, 2)), D((5,)), D((5,)), D((4,)), D((4,)), D((3, 3)), D((3, 3)), D((4, 7)), D((4, 7)), D((5,)),
        ],
        compiler_params=pltpu.CompilerParams(collective_id=0, has_side_effects=True, vmem_limit_bytes=66000000),
        name="conv_block",
    )

    def body(act_loc, w_loc, scale_loc, shift_loc, grad_loc):
        z, da, dw = call(act_loc[0].transpose(1, 2, 0, 3), w_loc[0].reshape(TAPS, LN, 1024), scale_loc, shift_loc, grad_loc[0].transpose(1, 2, 0, 3))
        return z.transpose(2, 0, 1, 3)[None], da.transpose(2, 0, 1, 3)[None], dw.reshape(1, 3, 3, LN, 1024)

    act_spec = P("stage", ("dp", "tp"))
    w_spec = P("stage", None, None, "tp")
    vec_spec = P("stage", "tp")
    grad_spec = P("stage", "dp", None, None, "tp")
    return jax.shard_map(body, mesh=mesh, in_specs=(act_spec, w_spec, vec_spec, vec_spec, grad_spec), out_specs=(grad_spec, act_spec, w_spec), check_vma=False)
```

time: 172 us -> 160 us (0.930)
  Pallas kernels: 163 us -> 152 us
    pallas_call x1, Pallas kernels: 163 us -> 152 us  [body(): call(act_loc[0].transpose(1, 2, 0, 3), w_loc[0].reshape(TAPS, LN, 1024),...]
where the time goes in v4:
time: 160 us
  Pallas kernels  152 us (95%)
  local copies, waits for them, and re-layouts  7.32 us (5%)
    pallas_call x1, Pallas kernels, body(): call(act_loc[0].transpose(1, 2, 0, 3), w_loc[0].reshape(TAPS, LN, 1024),...  152 us
    unnamed x9, local copies, waits for them, and re-layouts  7.32 us

profile of v4, /device:TPU:4, one launch (start us, length us, event | category | flops | bytes accessed | tf_op | source)
XLA Modules:
  0.0 160.1 jit_solution(17624593635590055271)
XLA Ops:
  0.6 152.1 %conv_block.1 = (bf16[28,28,8,256]{3,2,1,0:T(8,128)(2,1)}, bf16[28,28,2,512]{3,2,1,0:T(2,128)(2,1)}, f32[9,128,1024]{2,1,0:T(8,128)}) custom-call(bf16[28,28,2,512]{3,2,1,0:T(2,128)(2,1)} %bitcast.21, bf16[9,128,1024]{2,1,0:T(8,128)(2,1)} %bitcast.19, f32[1,256]{1,0:T(1,128)} %sc.1, f32[1,256]{1,0:T(1,128)} %sh.1, bf16[28,28,8,256]{3,2,1,0:T(8,128)(2,1)} %bitcast.18), custom_call_target="tpu_custom_call" | custom-call | tf_op jit(solution)/shard_map/conv_block/pallas_call | solution.py:416
  152.8 0.0 slice-start
  152.8 0.0 copy-start
  152.8 0.0 slice-start.1
  152.8 4.0 %copy.11 = bf16[1,8,28,28,256]{4,1,3,2,0:T(8,128)(2,1)} copy(bf16[1,8,28,28,256]{4,1,3,2,0:T(8,128)(2,1)} %bitcast.17) | data formatting | bytes 6422528
  156.8 0.0 copy-done
  156.8 1.2 copy.12
  157.9 0.0 slice-done
  157.9 0.0 slice-done.1
  157.9 2.2 %copy.13 = f32[1,3,3,128,1024]{4,3,2,1,0:T(8,128)} copy(f32[1,3,3,128,1024]{4,3,2,1,0:T(8,128)S(1)} %bitcast.16) | data formatting | bytes 9437184
  (1 shorter events, 0.0 us)
Async XLA Ops:
  152.8 5.2 %slice-start = ((s8[4718592]{0:T(1024)(128)(4,1)}), s8[4194304]{0:T(1024)(128)(4,1)S(1)}, s32[]{:S(2)}) async-start(s8[4718592]{0:T(1024)(128)(4,1)} %bitcast.14), calls=%async_computation | async-start | bytes 8388608
  152.8 4.0 %copy-start = (bf16[28,28,2,512]{3,2,1,0:T(2,128)(2,1)S(1)}, bf16[28,28,2,512]{3,2,1,0:T(2,128)(2,1)}, u32[]{:S(2)}) copy-start(bf16[28,28,2,512]{3,2,1,0:T(2,128)(2,1)} %get-tuple-element.7) | copy-start | bytes 4816900
  152.8 5.1 %slice-start.1 = ((s8[4718592]{0:T(1024)(128)(4,1)}), s8[524288]{0:T(1024)(128)(4,1)S(1)}, s32[]{:S(2)}) async-start(s8[4718592]{0:T(1024)(128)(4,1)} %bitcast.14), calls=%async_computation.1 | async-start | bytes 1048576

commit v5 on v4

--- a/solution.py
+++ b/solution.py
@@ -10,9 +10,13 @@
 BF = jnp.bfloat16
 F32 = jnp.float32
 MESH = pl.DeviceIdType.MESH
-CH = 4
-CB = (0, 8, 15, 22, 28)
-GP = ((0, 8), (8, 7), (20, 8), (15, 5))
+CH = 7
+CB = (0, 5, 9, 13, 17, 21, 25, 28)
+GR = 4
+CX = 5
+GX = 4
+DT = ((1, 0), (1, 1), (1, 2), (2, 2))
+ZX = ((0, 0, 9), (2, 0, 6), (3, 0, 3), (3, 3, 3), (3, 6, 3))
 HW = 28
 HP = 30
 NB = 8
@@ -24,7 +28,7 @@
 
 
 def kernel(act, w, sc, sh, gz, z_out, da_out, dw_out, A, AC, KO, KCU, KT, DZ, GU, W, WR, ACC, DAO, ZB,
-           lsem, ksem_s, ksem_r, kc_s, kc_r, kc_l, as_s, ax_r, a_r, f_s, gs_s, gs_r, g2_s, g2_r, g3_s, g3_r, gd_s, gd_r, rel_s, rel_r,
+           lsem, ksem_s, ksem_r, kc_s, kc_r, kc_l, as_s, ax_s, ax_r, af_s, a_r, f_s, gs_s, gs_r, g_s, g_r, gd_s, gd_r, rel_s, rel_r,
            zx_s, zx_r, d_s, d_r, da_s, da_r, out_s):
     dp = lax.axis_index("dp")
     stage = lax.axis_index("stage")
@@ -85,11 +89,11 @@
     def a_direct(c):
         return remote(act.at[pl.ds(CB[c], CB[c + 1] - CB[c])], a_slot(t, c), as_s.at[c], a_r.at[3, c], stage=1)
 
-    def a_cross():
-        return remote(act.at[pl.ds(CB[3], CB[4] - CB[3])], a_slot(t, 3), as_s.at[4], ax_r.at[0], tp=xn)
-
-    def a_cross_fwd():
-        return remote(a_slot(xn, 3), a_slot(xn, 3), as_s.at[5], a_r.at[1, 3], stage=1)
+    def a_cross(c):
+        return remote(act.at[pl.ds(CB[c], CB[c + 1] - CB[c])], a_slot(t, c), ax_s.at[c - CX], ax_r.at[c - CX], tp=xn)
+
+    def a_cross_fwd(c):
+        return remote(a_slot(xn, c), a_slot(xn, c), af_s.at[c - CX], a_r.at[1, c], stage=1)
 
     def a_fwd(kind, c):
         if kind == 0:
@@ -107,30 +111,28 @@
     mine = al(LN * k, LN)
     theirs = al(LN * (1 - k), LN)
 
-    def g2(c):
-        return remote(g_rows(0, 7 * c, 7, 0, LN), g_rows(2, 7 * c, 7, mine, LN), g2_s.at[c], g2_r.at[c], tp=xn)
-
-    def g3(p):
-        return remote(g_rows(0, GP[p][0], GP[p][1], LN, LN), g_rows(3, GP[p][0], GP[p][1], mine, LN), g3_s.at[p], g3_r.at[p], tp=xn)
-
-    def g2_rel(lane):
-        return remote(g_rows(2, 0, HW, lane, LN), g_rows(2, 0, HW, lane, LN), rel_s.at[0], rel_r.at[0], tp=sib)
-
-    def g3_rel(p, lane):
-        return remote(g_rows(3, GP[p][0], GP[p][1], lane, LN), g_rows(3, GP[p][0], GP[p][1], lane, LN), rel_s.at[1 + p], rel_r.at[1 + p], tp=sib)
-
-    def gdet(leg, p):
-        r0, n = GP[p]
-        own = g_rows(0, r0, n, LN, LN)
-        a3 = g_rows(3, r0, n, mine, LN)
-        a2 = g_rows(2, r0, n, mine, LN)
+    def g_x(u, c):
+        return remote(g_rows(0, GR * c, GR, LN * (u - 2), LN), g_rows(u, GR * c, GR, mine, LN), g_s.at[u - 2, c], g_r.at[u - 2, c], tp=xn)
+
+    def g_rel(u, c, lane):
+        return remote(g_rows(u, GR * c, GR, lane, LN), g_rows(u, GR * c, GR, lane, LN), rel_s.at[u - 2, c], rel_r.at[u - 2, c], tp=sib)
+
+    def gdet(leg, c):
+        own = g_rows(0, GR * c, GR, LN, LN)
+        a3 = g_rows(3, GR * c, GR, mine, LN)
+        a2 = g_rows(2, GR * c, GR, mine, LN)
         src, dst, dev = ((own, a3, {"stage": 0}), (a3, a2, {"tp": xn}), (a2, a3, {"stage": 1}))[leg]
-        return remote(src, dst, gd_s.at[leg, p - 2], gd_r.at[leg, p - 2], **dev)
-
-    def det(leg, p):
+        return remote(src, dst, gd_s.at[leg, c], gd_r.at[leg, c], **dev)
+
+    def det(leg, q):
         src, dst = ((W, WR), (WR, W), (W, WR))[leg]
         dev = ({"stage": 0}, {"dp": 1 - dp}, {"stage": 1})[leg]
-        return remote(src.at[1, pl.ds(3 * p, 3)], dst.at[1, pl.ds(3 * p, 3)], d_s.at[leg, p], d_r.at[leg, p], **dev)
+        u, p = DT[q]
+        return remote(src.at[u, pl.ds(3 * p, 3)], dst.at[u, pl.ds(3 * p, 3)], d_s.at[leg, q], d_r.at[leg, q], **dev)
+
+    def zx(q):
+        u, p, n = ZX[q]
+        return remote(W.at[u, pl.ds(p, n)], WR.at[u, pl.ds(p, n)], zx_s.at[q], zx_r.at[q], dp=1 - dp)
 
     def da_copy(s, n):
         return remote(DAO.at[pl.ds(2 * n, 2), :, pl.ds(2 * s, 2), :],
@@ -139,11 +141,13 @@
 
     @pl.when(stage == 0)
     def _():
-        a_cross().start()
+        for c in range(CX, CH):
+            a_cross(c).start()
         for c in range(CH):
             a_direct(c).start()
-        a_cross().wait_recv()
-        a_cross_fwd().start()
+        for c in range(CX, CH):
+            a_cross(c).wait_recv()
+            a_cross_fwd(c).start()
         W[0] = jnp.zeros((TAPS, LN, BLK), F32)
 
         def zrow(h, carry):
@@ -157,23 +161,26 @@
             o.start()
         for o in outs:
             o.wait()
-        for leg in range(2):
-            for p in (2, 3):
-                gdet(leg, p).wait_recv()
-                gdet(leg + 1, p).start()
-        for leg, p in ((0, 0), (0, 1), (1, 0), (0, 2), (1, 1), (1, 2)):
-            det(leg, p).wait_recv()
-            det(leg + 1, p).start()
+        for c in range(GX):
+            gdet(0, c).wait_recv()
+            gdet(1, c).start()
         for c in range(CH):
             a_direct(c).wait_send()
-        a_cross().wait_send()
-        a_cross_fwd().wait_send()
-        for p in range(3):
-            det(1, p).wait_send()
-            det(2, p).wait_send()
-        for p in (2, 3):
-            gdet(1, p).wait_send()
-            gdet(2, p).wait_send()
+        for c in range(CX, CH):
+            a_cross(c).wait_send()
+            a_cross_fwd(c).wait_send()
+        for c in range(GX):
+            gdet(1, c).wait_recv()
+            gdet(2, c).start()
+        for leg, q in ((0, 0), (0, 1), (1, 0), (0, 2), (1, 1), (1, 2), (0, 3), (1, 3)):
+            det(leg, q).wait_recv()
+            det(leg + 1, q).start()
+        for q in range(4):
+            det(1, q).wait_send()
+            det(2, q).wait_send()
+        for c in range(GX):
+            gdet(1, c).wait_send()
+            gdet(2, c).wait_send()
         for src in range(4):
             for n in range(7):
                 remote(DAO.at[pl.ds(2 * n, 2), :, pl.ds(0, 2), :],
@@ -198,32 +205,39 @@
         for o in zcp:
             o.start()
         ACC[...] = jnp.zeros((14, RW, BLK), F32)
-
-        for c in range(CH):
+        W[...] = jnp.zeros((4, TAPS, LN, BLK), F32)
+        AC[0] = jnp.zeros((HP, NB, LN), BF)
+        AC[29] = jnp.zeros((HP, NB, LN), BF)
+
+        def forward_images(c):
             a_recv(3, t, c).wait_recv()
-            if c < 3:
+            if c < CX:
                 a_fwd(1, c).start()
             a_fwd(0, c).start()
-            if c == 0:
-                for o in loc:
-                    o.wait()
-                for o in zcp:
-                    o.wait()
-                for i, (u, lane, wd, src) in enumerate(kc_pieces(t, sib)):
-                    remote(w.at[:, :, pl.ds(al(src, LN), wd)], KCU.at[u, :, pl.ds(al(LN * (1 - k), LN), LN), pl.ds(lane, wd)],
-                           kc_s.at[i], kc_r.at[i], tp=sib).wait_recv()
-            if c == 1:
-                k_copy(1, t, pz).wait_recv()
-                k_z(pz).start()
-
-            def tr(tap, carry, c=c):
-                KT[c, pl.ds(tap * BLK, BLK)] = KCU[c, tap].T
+
+        def transpose(u):
+            def tr(tap, carry):
+                KT[u, pl.ds(tap * BLK, BLK)] = KCU[u, tap].T
                 return carry
 
             lax.fori_loop(0, TAPS, tr, 0)
 
-        k_z(pz2).wait_recv()
-        k_copy(0, t, sib).wait_recv()
+        forward_images(0)
+        for o in loc:
+            o.wait()
+        for o in zcp:
+            o.wait()
+        for i, (u, lane, wd, src) in enumerate(kc_pieces(t, sib)):
+            remote(w.at[:, :, pl.ds(al(src, LN), wd)], KCU.at[u, :, pl.ds(theirs, LN), pl.ds(lane, wd)],
+                   kc_s.at[i], kc_r.at[i], tp=sib).wait_recv()
+        transpose(0)
+        transpose(1)
+        forward_images(1)
+        k_copy(1, t, pz).wait_recv()
+        k_z(pz).start()
+        transpose(2)
+        forward_images(2)
+        transpose(3)
 
         def row(h, carry):
             lhs = jnp.concatenate([A[h + i, j:j + HW].reshape(RW, CIN) for i in range(3) for j in range(3)], axis=1)
@@ -236,43 +250,51 @@
             return carry
 
         z_cp = pltpu.make_async_copy(DZ, z_out, lsem.at[0])
-        ac_cp = pltpu.make_async_copy(A.at[:, :, :, pl.ds(al(LN * t, LN), LN)], AC, lsem.at[1])
         g_sib = remote(GU.at[0], GU.at[1], gs_s.at[0], gs_r.at[0], tp=sib)
 
         for c in range(CH):
+            if c + 3 < CH:
+                forward_images(c + 3)
+            if c == 0:
+                k_z(pz2).wait_recv()
+                k_copy(0, t, sib).wait_recv()
             a_recv(1, xn, c).wait_recv()
             a_fwd(2, c).start()
             a_recv(0, sib, c).wait_recv()
             a_recv(2, dg, c).wait_recv()
-            if c == CH - 1:
-                ac_cp.start()
-            lax.fori_loop(7 * c, 7 * c + 7, row, 0)
-            g2(c).start()
-        for p in (2, 3):
-            gdet(0, p).start()
+            new = pl.ds(1 + CB[c], CB[c + 1] - CB[c])
+            AC[new] = A[new, :, :, pl.ds(al(LN * t, LN), LN)]
+            lax.fori_loop(GR * c, GR * c + GR, row, 0)
+            if c < GX:
+                gdet(0, c).start()
+            if c == 1:
+                g_x(2, 0).start()
+            if c > 0:
+                g_x(2, c).start()
         g_sib.start()
         z_cp.start()
-        ac_cp.wait()
-
-        zx = {u: remote(W.at[u], WR.at[u], zx_s.at[u], zx_r.at[u], dp=1 - dp) for u in (0, 2, 3)}
-
-        def dw_unit(u):
-            W[u] = jnp.zeros((TAPS, LN, BLK), F32)
-
+
+        def dw_step(u, n):
+            h = n * 7
+            lhs = jnp.concatenate([AC[pl.ds(h + i, 7), j:j + HW].reshape(1568, LN) for i in range(3) for j in range(3)], axis=1)
+            rhs = GU[u, pl.ds(h + 1, 7), 1:29].reshape(1568, BLK)
+            p = lax.dot_general(lhs, rhs, (((0,), (0,)), ((), ())), preferred_element_type=F32)
+            W[u] += p.reshape(TAPS, LN, BLK)
+
+        def dw_steps(u, lo, hi):
             def step(n, carry):
-                h = n * 7
-                lhs = jnp.concatenate([AC[pl.ds(h + i, 7), j:j + HW].reshape(1568, LN) for i in range(3) for j in range(3)], axis=1)
-                rhs = GU[u, pl.ds(h + 1, 7), 1:29].reshape(1568, BLK)
-                p = lax.dot_general(lhs, rhs, (((0,), (0,)), ((), ())), preferred_element_type=F32)
-                W[u] += p.reshape(TAPS, LN, BLK)
+                dw_step(u, n)
                 return carry
 
-            lax.fori_loop(0, 4, step, 0)
-            if u == 1:
-                for p in range(3):
-                    det(0, p).start()
-            else:
-                zx[u].start()
+            lax.fori_loop(lo, hi, step, 0)
+
+        def dw_send(u):
+            for q, d in enumerate(DT):
+                if d[0] == u:
+                    det(0, q).start()
+            for q, d in enumerate(ZX):
+                if d[0] == u:
+                    zx(q).start()
 
         def da_rows(u, n):
             h = 14 * k + 2 * n
@@ -295,11 +317,12 @@
                     for i, s in enumerate(starts)]
 
         def dw_final(u):
-            if u == 1:
-                for p in range(3):
-                    det(2, p).wait_recv()
-            else:
-                zx[u].wait_recv()
+            for q, d in enumerate(DT):
+                if d[0] == u:
+                    det(2, q).wait_recv()
+            for q, d in enumerate(ZX):
+                if d[0] == u:
+                    zx(q).wait_recv()
 
             def add(q, carry):
                 WR[u, q] += W[u, q]
@@ -309,11 +332,14 @@
             for o in dw_out_cp(u):
                 o.start()
 
-        dw_unit(0)
+        dw_steps(0, 0, 4)
+        dw_send(0)
         g_sib.wait_recv()
-        dw_unit(1)
+        dw_steps(1, 0, 4)
+        dw_send(1)
         da_unit(0)
         da_unit(1)
+
         def last(n, carry):
             v = ACC[pl.ds(2 * n, 2)].reshape(448, BLK) + da_rows(3, n)
             DAO[pl.ds(2 * n, 2)] = v.astype(BF).reshape(2, HW, NB, BLK)
@@ -321,42 +347,51 @@
                 da_copy(s, n).start()
             return carry
 
-        def g3_arrive(p):
-            if p < 2:
-                g3(p).wait_recv()
-            else:
-                gdet(2, p).wait_recv()
-            g3_rel(p, mine).start()
-            g3_rel(p, theirs).wait_recv()
-
+        def arrive(u, lo, hi):
+            for c in range(lo, hi):
+                if u == 3 and c < GX:
+                    gdet(2, c).wait_recv()
+                else:
+                    g_x(u, c).wait_recv()
+                g_rel(u, c, mine).start()
+            for c in range(lo, hi):
+                g_rel(u, c, theirs).wait_recv()
+
+        arrive(2, 0, 4)
+        dw_steps(2, 0, 2)
+        arrive(2, 4, 6)
+        dw_steps(2, 2, 3)
         for c in range(CH):
-            g2(c).wait_send()
-        g3(0).start()
-        for c in range(CH):
-            g2(c).wait_recv()
-        g2_rel(mine).start()
-        g2_rel(theirs).wait_recv()
-        dw_unit(2)
-        g3(0).wait_send()
-        g3(1).start()
+            g_x(2, c).wait_send()
+        for c in range(GX, CH):
+            g_x(3, c).start()
+        arrive(2, 6, 7)
+        dw_steps(2, 3, 4)
+        dw_send(2)
         da_unit(2)
-        g3_arrive(2)
+        arrive(3, 0, 4)
+
+        @pl.when(k == 0)
+        def _():
+            lax.fori_loop(0, 7, last, 0)
+
+        dw_steps(3, 0, 2)
+        dw_final(0)
+        arrive(3, 4, 6)
+        dw_steps(3, 2, 3)
+
+        @pl.when(k == 1)
+        def _():
+            lax.fori_loop(0, 4, last, 0)
+
+        arrive(3, 6, 7)
+        dw_steps(3, 3, 4)
+        dw_send(3)
 
         @pl.when(k == 1)
         def _():
             lax.fori_loop(4, 7, last, 0)
 
-        g3_arrive(0)
-
-        @pl.when(k == 0)
-        def _():
-            lax.fori_loop(0, 3, last, 0)
-
-        dw_final(0)
-        g3_arrive(3)
-        g3_arrive(1)
-        dw_unit(3)
-        lax.fori_loop(3 - 3 * k, 7 - 3 * k, last, 0)
         dw_final(1)
         for u in range(2, 4):
             dw_final(u)
@@ -365,10 +400,10 @@
         for u in range(4):
             for o in dw_out_cp(u):
                 o.wait()
-            if u != 1:
-                zx[u].wait_send()
-        for p in range(3):
-            det(0, p).wait_send()
+        for q in range(4):
+            det(0, q).wait_send()
+        for q in range(5):
+            zx(q).wait_send()
         k_copy(1, pz, t).wait_send()
         k_z(pz).wait_send()
         k_copy(0, sib, t).wait_send()
@@ -377,15 +412,15 @@
                    kc_s.at[i], kc_r.at[i], tp=sib).wait_send()
         for c in range(CH):
             for kind in range(3):
-                if kind != 1 or c < 3:
+                if kind != 1 or c < CX:
                     a_fwd(kind, c).wait_send()
+            g_rel(2, c, mine).wait_send()
+            g_rel(3, c, mine).wait_send()
+            if c < GX:
+                gdet(0, c).wait_send()
+            else:
+                g_x(3, c).wait_send()
         g_sib.wait_send()
-        g2_rel(mine).wait_send()
-        g3(1).wait_send()
-        for p in (2, 3):
-            gdet(0, p).wait_send()
-        for p in range(4):
-            g3_rel(p, mine).wait_send()
         for s in range(4):
             for n in range(7):
                 da_copy(s, n).wait_send()
@@ -405,8 +440,8 @@
             V((HP, HP, NB, CIN), BF), V((HP, HP, NB, LN), BF), V((TAPS, CIN, BLK), BF), V((4, TAPS, BLK, BLK), BF), V((4, 2304, BLK), BF),
             V((HW, HW, NB, BLK), BF), V((4, HP, HP, NB, BLK), BF), V((4, TAPS, LN, BLK), F32), V((4, TAPS, LN, BLK), F32),
             V((14, RW, BLK), F32), V((14, HW, NB, BLK), BF), V((7, HW, 2, CIN), BF),
-            D((2,)), D((3,)), D((3,)), D((6,)), D((6,)), D((6,)), D((6,)), D((1,)), D((4, 4)), D((3, 4)), D((1,)), D((1,)), D((4,)), D((4,)),
-            D((2,)), D((2,)), D((3, 2)), D((3, 2)), D((5,)), D((5,)), D((4,)), D((4,)), D((3, 3)), D((3, 3)), D((4, 7)), D((4, 7)), D((5,)),
+            D((2,)), D((3,)), D((3,)), D((6,)), D((6,)), D((6,)), D((CH,)), D((2,)), D((2,)), D((2,)), D((4, CH)), D((3, CH)), D((1,)), D((1,)),
+            D((2, CH)), D((2, CH)), D((3, GX)), D((3, GX)), D((2, CH)), D((2, CH)), D((5,)), D((5,)), D((3, 4)), D((3, 4)), D((4, 7)), D((4, 7)), D((5,)),
         ],
         compiler_params=pltpu.CompilerParams(collective_id=0, has_side_effects=True, vmem_limit_bytes=66000000),
         name="conv_block",

time: 160 us -> 156 us (0.975)
  Pallas kernels: 152 us -> 147 us
    pallas_call x1, Pallas kernels: 152 us -> 147 us  [body(): call(act_loc[0].transpose(1, 2, 0, 3), w_loc[0].reshape(TAPS, LN, 1024),...]
where the time goes in v5:
time: 156 us; the launch traced here: 155 us
  Pallas kernels  147 us (94%)
  local copies, waits for them, and re-layouts  7.32 us (5%)
    pallas_call x1, Pallas kernels, body(): call(act_loc[0].transpose(1, 2, 0, 3), w_loc[0].reshape(TAPS, LN, 1024),...  147 us
    unnamed x9, local copies, waits for them, and re-layouts  7.32 us

profile of v5, /device:TPU:4, one launch (start us, length us, event | category | flops | bytes accessed | tf_op | source)
XLA Modules:
  0.0 154.8 jit_solution(11065228577561630073)
XLA Ops:
  0.6 146.8 %conv_block.1 = (bf16[28,28,8,256]{3,2,1,0:T(8,128)(2,1)}, bf16[28,28,2,512]{3,2,1,0:T(2,128)(2,1)}, f32[9,128,1024]{2,1,0:T(8,128)}) custom-call(bf16[28,28,2,512]{3,2,1,0:T(2,128)(2,1)} %bitcast.21, bf16[9,128,1024]{2,1,0:T(8,128)(2,1)} %bitcast.19, f32[1,256]{1,0:T(1,128)} %sc.1, f32[1,256]{1,0:T(1,128)} %sh.1, bf16[28,28,8,256]{3,2,1,0:T(8,128)(2,1)} %bitcast.18), custom_call_target="tpu_custom_call" | custom-call | tf_op jit(solution)/shard_map/conv_block/pallas_call | solution.py:451
  147.4 0.0 slice-start
  147.4 0.0 copy-start
  147.5 0.0 slice-start.1
  147.5 4.0 %copy.11 = bf16[1,8,28,28,256]{4,1,3,2,0:T(8,128)(2,1)} copy(bf16[1,8,28,28,256]{4,1,3,2,0:T(8,128)(2,1)} %bitcast.17) | data formatting | bytes 6422528
  151.4 0.0 copy-done
  151.4 1.2 copy.12
  152.6 0.0 slice-done
  152.6 0.0 slice-done.1
  152.6 2.2 %copy.13 = f32[1,3,3,128,1024]{4,3,2,1,0:T(8,128)} copy(f32[1,3,3,128,1024]{4,3,2,1,0:T(8,128)S(1)} %bitcast.16) | data formatting | bytes 9437184
  (1 shorter events, 0.0 us)
Async XLA Ops:
  147.4 5.2 %slice-start = ((s8[4718592]{0:T(1024)(128)(4,1)}), s8[4194304]{0:T(1024)(128)(4,1)S(1)}, s32[]{:S(2)}) async-start(s8[4718592]{0:T(1024)(128)(4,1)} %bitcast.14), calls=%async_computation | async-start | bytes 8388608
  147.4 4.0 %copy-start = (bf16[28,28,2,512]{3,2,1,0:T(2,128)(2,1)S(1)}, bf16[28,28,2,512]{3,2,1,0:T(2,128)(2,1)}, u32[]{:S(2)}) copy-start(bf16[28,28,2,512]{3,2,1,0:T(2,128)(2,1)} %get-tuple-element.7) | copy-start | bytes 4816900
  147.5 5.1 %slice-start.1 = ((s8[4718592]{0:T(1024)(128)(4,1)}), s8[524288]{0:T(1024)(128)(4,1)S(1)}, s32[]{:S(2)}) async-start(s8[4718592]{0:T(1024)(128)(4,1)} %bitcast.14), calls=%async_computation.1 | async-start | bytes 1048576

commit v6 on v5

--- a/solution.py
+++ b/solution.py
@@ -27,7 +27,7 @@
 CIN = 512
 
 
-def kernel(act, w, sc, sh, gz, z_out, da_out, dw_out, A, AC, KO, KCU, KT, DZ, GU, W, WR, ACC, DAO, ZB,
+def kernel(act, w, sc, sh, gz, z_out, da_out, dw_out, A, AC, KO, KCU, KT, DZ, GU, W, WR, ACC, DAO, ZB, L, DAL,
            lsem, ksem_s, ksem_r, kc_s, kc_r, kc_l, as_s, ax_s, ax_r, af_s, a_r, f_s, gs_s, gs_r, g_s, g_r, gd_s, gd_r, rel_s, rel_r,
            zx_s, zx_r, d_s, d_r, da_s, da_r, out_s):
     dp = lax.axis_index("dp")
@@ -84,7 +84,7 @@
                 (3, 0, LN, base + LN), (3, LN, LN, base + 384))
 
     def a_slot(src, c):
-        return A.at[pl.ds(1 + CB[c], CB[c + 1] - CB[c]), pl.ds(1, HW), pl.ds(2 * src, 2), :]
+        return L.at[src, pl.ds(CB[c], CB[c + 1] - CB[c])]
 
     def a_direct(c):
         return remote(act.at[pl.ds(CB[c], CB[c + 1] - CB[c])], a_slot(t, c), as_s.at[c], a_r.at[3, c], stage=1)
@@ -135,9 +135,7 @@
         return remote(W.at[u, pl.ds(p, n)], WR.at[u, pl.ds(p, n)], zx_s.at[q], zx_r.at[q], dp=1 - dp)
 
     def da_copy(s, n):
-        return remote(DAO.at[pl.ds(2 * n, 2), :, pl.ds(2 * s, 2), :],
-                      da_out.at[pl.ds(14 * k + 2 * n, 2), :, :, pl.ds(al(BLK * x, BLK), BLK)],
-                      da_s.at[s, n], da_r.at[t, n], stage=0, tp=s)
+        return remote(DAO.at[s, pl.ds(2 * n, 2)], DAL.at[x, pl.ds(14 * k + 2 * n, 2)], da_s.at[s, n], da_r.at[t, n], stage=0, tp=s)
 
     @pl.when(stage == 0)
     def _():
@@ -181,11 +179,16 @@
         for c in range(GX):
             gdet(1, c).wait_send()
             gdet(2, c).wait_send()
-        for src in range(4):
+        outs = []
+        for src in (0, 2, 1, 3):
             for n in range(7):
-                remote(DAO.at[pl.ds(2 * n, 2), :, pl.ds(0, 2), :],
-                       da_out.at[pl.ds(14 * (src % 2) + 2 * n, 2), :, :, pl.ds(BLK * (src // 2), BLK)],
-                       da_s.at[0, n], da_r.at[src, n], stage=0, tp=0).wait_recv()
+                rows = pl.ds(14 * (src % 2) + 2 * n, 2)
+                remote(DAO.at[0, pl.ds(2 * n, 2)], DAL.at[src // 2, rows], da_s.at[0, n], da_r.at[src, n], stage=0, tp=0).wait_recv()
+                o = pltpu.make_async_copy(DAL.at[src // 2, rows], da_out.at[rows, :, :, pl.ds(BLK * (src // 2), BLK)], da_s.at[src, n])
+                o.start()
+                outs.append(o)
+        for o in outs:
+            o.wait()
 
     @pl.when(stage == 1)
     def _():
@@ -239,6 +242,10 @@
         forward_images(2)
         transpose(3)
 
+        def merge(h, carry):
+            A[h + 1, 1:29] = jnp.concatenate([L[s, h] for s in range(4)], axis=1)
+            return carry
+
         def row(h, carry):
             lhs = jnp.concatenate([A[h + i, j:j + HW].reshape(RW, CIN) for i in range(3) for j in range(3)], axis=1)
             pre = jnp.dot(lhs, KO[...].reshape(4608, BLK), preferred_element_type=F32)
@@ -262,6 +269,7 @@
             a_fwd(2, c).start()
             a_recv(0, sib, c).wait_recv()
             a_recv(2, dg, c).wait_recv()
+            lax.fori_loop(CB[c], CB[c + 1], merge, 0)
             new = pl.ds(1 + CB[c], CB[c + 1] - CB[c])
             AC[new] = A[new, :, :, pl.ds(al(LN * t, LN), LN)]
             lax.fori_loop(GR * c, GR * c + GR, row, 0)
@@ -342,7 +350,9 @@
 
         def last(n, carry):
             v = ACC[pl.ds(2 * n, 2)].reshape(448, BLK) + da_rows(3, n)
-            DAO[pl.ds(2 * n, 2)] = v.astype(BF).reshape(2, HW, NB, BLK)
+            v = v.astype(BF).reshape(2, HW, NB, BLK)
+            for s in range(4):
+                DAO[s, pl.ds(2 * n, 2)] = v[:, :, 2 * s:2 * s + 2, :]
             for s in range(4):
                 da_copy(s, n).start()
             return carry
@@ -439,7 +449,7 @@
         scratch_shapes=[
             V((HP, HP, NB, CIN), BF), V((HP, HP, NB, LN), BF), V((TAPS, CIN, BLK), BF), V((4, TAPS, BLK, BLK), BF), V((4, 2304, BLK), BF),
             V((HW, HW, NB, BLK), BF), V((4, HP, HP, NB, BLK), BF), V((4, TAPS, LN, BLK), F32), V((4, TAPS, LN, BLK), F32),
-            V((14, RW, BLK), F32), V((14, HW, NB, BLK), BF), V((7, HW, 2, CIN), BF),
+            V((14, RW, BLK), F32), V((4, 14, HW, 2, BLK), BF), V((7, HW, 2, CIN), BF), V((4, HW, HW, 2, CIN), BF), V((2, HW, HW, 2, BLK), BF),
             D((2,)), D((3,)), D((3,)), D((6,)), D((6,)), D((6,)), D((CH,)), D((2,)), D((2,)), D((2,)), D((4, CH)), D((3, CH)), D((1,)), D((1,)),
             D((2, CH)), D((2, CH)), D((3, GX)), D((3, GX)), D((2, CH)), D((2, CH)), D((5,)), D((5,)), D((3, 4)), D((3, 4)), D((4, 7)), D((4, 7)), D((5,)),
         ],

time: 156 us -> 160 us (1.026)
  Pallas kernels: 147 us -> 151 us
    pallas_call x1, Pallas kernels: 147 us -> 151 us  [body(): call(act_loc[0].transpose(1, 2, 0, 3), w_loc[0].reshape(TAPS, LN, 1024),...]
where the time goes in v6:
time: 160 us; the launch traced here: 159 us
  Pallas kernels  151 us (94%)
  local copies, waits for them, and re-layouts  7.32 us (5%)
    pallas_call x1, Pallas kernels, body(): call(act_loc[0].transpose(1, 2, 0, 3), w_loc[0].reshape(TAPS, LN, 1024),...  151 us
    unnamed x9, local copies, waits for them, and re-layouts  7.32 us

profile of v6, /device:TPU:4, one launch (start us, length us, event | category | flops | bytes accessed | tf_op | source)
XLA Modules:
  0.0 158.6 jit_solution(5890470987633906430)
XLA Ops:
  0.6 150.6 %conv_block.1 = (bf16[28,28,8,256]{3,2,1,0:T(8,128)(2,1)}, bf16[28,28,2,512]{3,2,1,0:T(2,128)(2,1)}, f32[9,128,1024]{2,1,0:T(8,128)}) custom-call(bf16[28,28,2,512]{3,2,1,0:T(2,128)(2,1)} %bitcast.21, bf16[9,128,1024]{2,1,0:T(8,128)(2,1)} %bitcast.19, f32[1,256]{1,0:T(1,128)} %sc.1, f32[1,256]{1,0:T(1,128)} %sh.1, bf16[28,28,8,256]{3,2,1,0:T(8,128)(2,1)} %bitcast.18), custom_call_target="tpu_custom_call" | custom-call | tf_op jit(solution)/shard_map/conv_block/pallas_call | solution.py:461
  151.2 0.0 slice-start
  151.2 0.0 copy-start
  151.2 0.0 slice-start.1
  151.2 4.0 %copy.11 = bf16[1,8,28,28,256]{4,1,3,2,0:T(8,128)(2,1)} copy(bf16[1,8,28,28,256]{4,1,3,2,0:T(8,128)(2,1)} %bitcast.17) | data formatting | bytes 6422528
  155.2 0.0 copy-done
  155.2 1.2 copy.12
  156.4 0.0 slice-done
  156.4 0.0 slice-done.1
  156.4 2.2 %copy.13 = f32[1,3,3,128,1024]{4,3,2,1,0:T(8,128)} copy(f32[1,3,3,128,1024]{4,3,2,1,0:T(8,128)S(1)} %bitcast.16) | data formatting | bytes 9437184
  (1 shorter events, 0.0 us)
Async XLA Ops:
  151.2 5.2 %slice-start = ((s8[4718592]{0:T(1024)(128)(4,1)}), s8[4194304]{0:T(1024)(128)(4,1)S(1)}, s32[]{:S(2)}) async-start(s8[4718592]{0:T(1024)(128)(4,1)} %bitcast.14), calls=%async_computation | async-start | bytes 8388608
  151.2 4.0 %copy-start = (bf16[28,28,2,512]{3,2,1,0:T(2,128)(2,1)S(1)}, bf16[28,28,2,512]{3,2,1,0:T(2,128)(2,1)}, u32[]{:S(2)}) copy-start(bf16[28,28,2,512]{3,2,1,0:T(2,128)(2,1)} %get-tuple-element.7) | copy-start | bytes 4816900
  151.2 5.1 %slice-start.1 = ((s8[4718592]{0:T(1024)(128)(4,1)}), s8[524288]{0:T(1024)(128)(4,1)S(1)}, s32[]{:S(2)}) async-start(s8[4718592]{0:T(1024)(128)(4,1)} %bitcast.14), calls=%async_computation.1 | async-start | bytes 1048576

commit v7 on v5

--- a/solution.py
+++ b/solution.py
@@ -28,7 +28,7 @@
 
 
 def kernel(act, w, sc, sh, gz, z_out, da_out, dw_out, A, AC, KO, KCU, KT, DZ, GU, W, WR, ACC, DAO, ZB,
-           lsem, ksem_s, ksem_r, kc_s, kc_r, kc_l, as_s, ax_s, ax_r, af_s, a_r, f_s, gs_s, gs_r, g_s, g_r, gd_s, gd_r, rel_s, rel_r,
+           lsem, ksem_s, ksem_r, kx_s, kx_r, kz_s, kz_r, kc_s, kc_r, kc_l, as_s, ax_s, ax_r, af_s, a_r, f_s, gs_s, gs_r, g_s, g_r, gd_s, gd_r, rel_s, rel_r,
            zx_s, zx_r, d_s, d_r, da_s, da_r, out_s):
     dp = lax.axis_index("dp")
     stage = lax.axis_index("stage")
@@ -76,8 +76,13 @@
     def k_copy(rel, peer, src_tp):
         return remote(w.at[:, :, pl.ds(al(BLK * peer, BLK), BLK)], k_slot(src_tp), ksem_s.at[rel], ksem_r.at[rel], tp=peer)
 
-    def k_z(src_tp):
-        return remote(k_slot(src_tp), k_slot(src_tp), ksem_s.at[2], ksem_r.at[2], dp=1 - dp)
+    def k_x(peer, src_tp, p):
+        taps = pl.ds(3 * p, 3)
+        return remote(w.at[taps, :, pl.ds(al(BLK * peer, BLK), BLK)], KO.at[taps, pl.ds(al(LN * src_tp, LN), LN), :], kx_s.at[p], kx_r.at[p], tp=peer)
+
+    def k_z(src_tp, p):
+        slot = KO.at[pl.ds(3 * p, 3), pl.ds(al(LN * src_tp, LN), LN), :]
+        return remote(slot, slot, kz_s.at[p], kz_r.at[p], dp=1 - dp)
 
     def kc_pieces(own, other):
         return ((0, 0, BLK, BLK * own), (1, 0, BLK, BLK * other), (2, 0, LN, base), (2, LN, LN, base + BLK),
@@ -189,7 +194,8 @@
 
     @pl.when(stage == 1)
     def _():
-        k_copy(1, pz, t).start()
+        for p in range(3):
+            k_x(pz, t, p).start()
         k_copy(0, sib, t).start()
         for i, (u, lane, wd, src) in enumerate(kc_pieces(sib, t)):
             remote(w.at[:, :, pl.ds(al(src, LN), wd)], KCU.at[u, :, pl.ds(al(LN * k, LN), LN), pl.ds(lane, wd)],
@@ -222,7 +228,13 @@
 
             lax.fori_loop(0, TAPS, tr, 0)
 
+        def weights_on(p):
+            k_x(t, pz, p).wait_recv()
+            k_z(pz, p).start()
+
+        weights_on(0)
         forward_images(0)
+        weights_on(1)
         for o in loc:
             o.wait()
         for o in zcp:
@@ -231,10 +243,9 @@
             remote(w.at[:, :, pl.ds(al(src, LN), wd)], KCU.at[u, :, pl.ds(theirs, LN), pl.ds(lane, wd)],
                    kc_s.at[i], kc_r.at[i], tp=sib).wait_recv()
         transpose(0)
+        forward_images(1)
+        weights_on(2)
         transpose(1)
-        forward_images(1)
-        k_copy(1, t, pz).wait_recv()
-        k_z(pz).start()
         transpose(2)
         forward_images(2)
         transpose(3)
@@ -256,7 +267,8 @@
             if c + 3 < CH:
                 forward_images(c + 3)
             if c == 0:
-                k_z(pz2).wait_recv()
+                for p in range(3):
+                    k_z(pz2, p).wait_recv()
                 k_copy(0, t, sib).wait_recv()
             a_recv(1, xn, c).wait_recv()
             a_fwd(2, c).start()
@@ -301,12 +313,12 @@
             lhs = jnp.concatenate([GU[u, pl.ds(h + 2 - i, 2), 2 - j:HP - j].reshape(448, BLK) for i in range(3) for j in range(3)], axis=1)
             return jnp.dot(lhs, KT[u], preferred_element_type=F32)
 
-        def da_unit(u):
+        def da_unit(u, count=7):
             def step(n, carry):
                 ACC[pl.ds(2 * n, 2)] += da_rows(u, n).reshape(2, RW, BLK)
                 return carry
 
-            lax.fori_loop(0, 7, step, 0)
+            lax.fori_loop(0, count, step, 0)
 
         dw_dst = ((BLK * t,), (BLK * sib,), (base, base + BLK), (base + LN, base + 384))
 
@@ -338,7 +350,6 @@
         dw_steps(1, 0, 4)
         dw_send(1)
         da_unit(0)
-        da_unit(1)
 
         def last(n, carry):
             v = ACC[pl.ds(2 * n, 2)].reshape(448, BLK) + da_rows(3, n)
@@ -347,51 +358,42 @@
                 da_copy(s, n).start()
             return carry
 
-        def arrive(u, lo, hi):
+        def take(u, lo, hi):
             for c in range(lo, hi):
                 if u == 3 and c < GX:
                     gdet(2, c).wait_recv()
                 else:
                     g_x(u, c).wait_recv()
                 g_rel(u, c, mine).start()
+
+        def got(u, lo, hi):
             for c in range(lo, hi):
                 g_rel(u, c, theirs).wait_recv()
 
-        arrive(2, 0, 4)
-        dw_steps(2, 0, 2)
-        arrive(2, 4, 6)
-        dw_steps(2, 2, 3)
+        take(2, 0, 6)
+        got(2, 0, 6)
+        dw_steps(2, 0, 3)
         for c in range(CH):
             g_x(2, c).wait_send()
         for c in range(GX, CH):
             g_x(3, c).start()
-        arrive(2, 6, 7)
+        take(2, 6, 7)
+        got(2, 6, 7)
         dw_steps(2, 3, 4)
         dw_send(2)
-        da_unit(2)
-        arrive(3, 0, 4)
-
-        @pl.when(k == 0)
-        def _():
-            lax.fori_loop(0, 7, last, 0)
-
-        dw_steps(3, 0, 2)
+        take(3, 0, 4)
+        got(3, 0, 4)
+        dw_steps(3, 0, 2 * k)
+        da_unit(1)
+        da_unit(2, 7 - 7 * k)
+        take(3, 4, 7)
+        lax.fori_loop(0, 7 - 7 * k, last, 0)
+        got(3, 4, 7)
+        dw_steps(3, 2 * k, 4)
+        dw_send(3)
+        da_unit(2, 7 * k)
+        lax.fori_loop(0, 7 * k, last, 0)
         dw_final(0)
-        arrive(3, 4, 6)
-        dw_steps(3, 2, 3)
-
-        @pl.when(k == 1)
-        def _():
-            lax.fori_loop(0, 4, last, 0)
-
-        arrive(3, 6, 7)
-        dw_steps(3, 3, 4)
-        dw_send(3)
-
-        @pl.when(k == 1)
-        def _():
-            lax.fori_loop(4, 7, last, 0)
-
         dw_final(1)
         for u in range(2, 4):
             dw_final(u)
@@ -404,8 +406,9 @@
             det(0, q).wait_send()
         for q in range(5):
             zx(q).wait_send()
-        k_copy(1, pz, t).wait_send()
-        k_z(pz).wait_send()
+        for p in range(3):
+            k_x(pz, t, p).wait_send()
+            k_z(pz, p).wait_send()
         k_copy(0, sib, t).wait_send()
         for i, (u, lane, wd, src) in enumerate(kc_pieces(sib, t)):
             remote(w.at[:, :, pl.ds(al(src, LN), wd)], KCU.at[u, :, pl.ds(al(LN * k, LN), LN), pl.ds(lane, wd)],
@@ -440,7 +443,7 @@
             V((HP, HP, NB, CIN), BF), V((HP, HP, NB, LN), BF), V((TAPS, CIN, BLK), BF), V((4, TAPS, BLK, BLK), BF), V((4, 2304, BLK), BF),
             V((HW, HW, NB, BLK), BF), V((4, HP, HP, NB, BLK), BF), V((4, TAPS, LN, BLK), F32), V((4, TAPS, LN, BLK), F32),
             V((14, RW, BLK), F32), V((14, HW, NB, BLK), BF), V((7, HW, 2, CIN), BF),
-            D((2,)), D((3,)), D((3,)), D((6,)), D((6,)), D((6,)), D((CH,)), D((2,)), D((2,)), D((2,)), D((4, CH)), D((3, CH)), D((1,)), D((1,)),
+            D((2,)), D((3,)), D((3,)), D((3,)), D((3,)), D((3,)), D((3,)), D((6,)), D((6,)), D((6,)), D((CH,)), D((2,)), D((2,)), D((2,)), D((4, CH)), D((3, CH)), D((1,)), D((1,)),
             D((2, CH)), D((2, CH)), D((3, GX)), D((3, GX)), D((2, CH)), D((2, CH)), D((5,)), D((5,)), D((3, 4)), D((3, 4)), D((4, 7)), D((4, 7)), D((5,)),
         ],
         compiler_params=pltpu.CompilerParams(collective_id=0, has_side_effects=True, vmem_limit_bytes=66000000),

time: 156 us -> 152 us (0.974)
  Pallas kernels: 147 us -> 144 us
    pallas_call x1, Pallas kernels: 147 us -> 144 us  [body(): call(act_loc[0].transpose(1, 2, 0, 3), w_loc[0].reshape(TAPS, LN, 1024),...]
where the time goes in v7:
time: 152 us
  Pallas kernels  144 us (95%)
  local copies, waits for them, and re-layouts  7.32 us (5%)
    pallas_call x1, Pallas kernels, body(): call(act_loc[0].transpose(1, 2, 0, 3), w_loc[0].reshape(TAPS, LN, 1024),...  144 us
    unnamed x9, local copies, waits for them, and re-layouts  7.32 us

profile of v7, /device:TPU:4, one launch (start us, length us, event | category | flops | bytes accessed | tf_op | source)
XLA Modules:
  0.0 151.8 jit_solution(5409641981743737103)
XLA Ops:
  0.6 143.8 %conv_block.1 = (bf16[28,28,8,256]{3,2,1,0:T(8,128)(2,1)}, bf16[28,28,2,512]{3,2,1,0:T(2,128)(2,1)}, f32[9,128,1024]{2,1,0:T(8,128)}) custom-call(bf16[28,28,2,512]{3,2,1,0:T(2,128)(2,1)} %bitcast.21, bf16[9,128,1024]{2,1,0:T(8,128)(2,1)} %bitcast.19, f32[1,256]{1,0:T(1,128)} %sc.1, f32[1,256]{1,0:T(1,128)} %sh.1, bf16[28,28,8,256]{3,2,1,0:T(8,128)(2,1)} %bitcast.18), custom_call_target="tpu_custom_call" | custom-call | tf_op jit(solution)/shard_map/conv_block/pallas_call | solution.py:454
  144.4 0.0 slice-start
  144.4 0.0 copy-start
  144.4 0.0 slice-start.1
  144.5 4.0 %copy.11 = bf16[1,8,28,28,256]{4,1,3,2,0:T(8,128)(2,1)} copy(bf16[1,8,28,28,256]{4,1,3,2,0:T(8,128)(2,1)} %bitcast.17) | data formatting | bytes 6422528
  148.4 0.0 copy-done
  148.4 1.2 copy.12
  149.6 0.0 slice-done
  149.6 0.0 slice-done.1
  149.6 2.2 %copy.13 = f32[1,3,3,128,1024]{4,3,2,1,0:T(8,128)} copy(f32[1,3,3,128,1024]{4,3,2,1,0:T(8,128)S(1)} %bitcast.16) | data formatting | bytes 9437184
  (1 shorter events, 0.0 us)
Async XLA Ops:
  144.4 5.2 %slice-start = ((s8[4718592]{0:T(1024)(128)(4,1)}), s8[4194304]{0:T(1024)(128)(4,1)S(1)}, s32[]{:S(2)}) async-start(s8[4718592]{0:T(1024)(128)(4,1)} %bitcast.14), calls=%async_computation | async-start | bytes 8388608
  144.4 4.0 %copy-start = (bf16[28,28,2,512]{3,2,1,0:T(2,128)(2,1)S(1)}, bf16[28,28,2,512]{3,2,1,0:T(2,128)(2,1)}, u32[]{:S(2)}) copy-start(bf16[28,28,2,512]{3,2,1,0:T(2,128)(2,1)} %get-tuple-element.7) | copy-start | bytes 4816900
  144.4 5.1 %slice-start.1 = ((s8[4718592]{0:T(1024)(128)(4,1)}), s8[524288]{0:T(1024)(128)(4,1)S(1)}, s32[]{:S(2)}) async-start(s8[4718592]{0:T(1024)(128)(4,1)} %bitcast.14), calls=%async_computation.1 | async-start | bytes 1048576

commit v8 on v7

--- a/solution.py
+++ b/solution.py
@@ -250,14 +250,16 @@
         forward_images(2)
         transpose(3)
 
-        def row(h, carry):
-            lhs = jnp.concatenate([A[h + i, j:j + HW].reshape(RW, CIN) for i in range(3) for j in range(3)], axis=1)
+        def rows(m, carry):
+            h = 2 * m
+            two = pl.ds(h, 2)
+            lhs = jnp.concatenate([A[pl.ds(h + i, 2), j:j + HW].reshape(2 * RW, CIN) for i in range(3) for j in range(3)], axis=1)
             pre = jnp.dot(lhs, KO[...].reshape(4608, BLK), preferred_element_type=F32)
             y = pre * sc[...] + sh[...]
-            d = DZ[h].reshape(RW, BLK).astype(F32)
+            d = DZ[two].reshape(2 * RW, BLK).astype(F32)
             g = jnp.where(y > 0, d * sc[...], 0.0).astype(BF)
-            DZ[h] = jnp.maximum(y, 0.0).astype(BF).reshape(HW, NB, BLK)
-            GU[0, h + 1, 1:29] = g.reshape(HW, NB, BLK)
+            DZ[two] = jnp.maximum(y, 0.0).astype(BF).reshape(2, HW, NB, BLK)
+            GU[0, pl.ds(h + 1, 2), 1:29] = g.reshape(2, HW, NB, BLK)
             return carry
 
         z_cp = pltpu.make_async_copy(DZ, z_out, lsem.at[0])
@@ -276,7 +278,7 @@
             a_recv(2, dg, c).wait_recv()
             new = pl.ds(1 + CB[c], CB[c + 1] - CB[c])
             AC[new] = A[new, :, :, pl.ds(al(LN * t, LN), LN)]
-            lax.fori_loop(GR * c, GR * c + GR, row, 0)
+            lax.fori_loop(2 * c, 2 * c + 2, rows, 0)
             if c < GX:
                 gdet(0, c).start()
             if c == 1:
@@ -452,6 +454,7 @@
 
     def body(act_loc, w_loc, scale_loc, shift_loc, grad_loc):
         z, da, dw = call(act_loc[0].transpose(1, 2, 0, 3), w_loc[0].reshape(TAPS, LN, 1024), scale_loc, shift_loc, grad_loc[0].transpose(1, 2, 0, 3))
+        z = jnp.maximum(z, 0.0)
         return z.transpose(2, 0, 1, 3)[None], da.transpose(2, 0, 1, 3)[None], dw.reshape(1, 3, 3, LN, 1024)
 
     act_spec = P("stage", ("dp", "tp"))

time: 152 us -> 150 us (0.987)
  local copies, waits for them, and re-layouts: 7.32 us -> 3.35 us
  other arithmetic: 0.01 us -> 3.97 us
  Pallas kernels: 144 us -> 142 us
    broadcast_in_dim x0 -> x1, other arithmetic: none -> 3.97 us  [body(): z.transpose(2, 0, 1, 3)[None]]
    unnamed x9 -> x8, local copies, waits for them, and re-layouts: 7.32 us -> 3.35 us
    pallas_call x1, Pallas kernels: 144 us -> 142 us  [body(): call(act_loc[0].transpose(1, 2, 0, 3), w_loc[0].reshape(TAPS, LN, 1024),...]
where the time goes in v8:
time: 150 us
  Pallas kernels  142 us (95%)
  other arithmetic  3.97 us (3%)
  local copies, waits for them, and re-layouts  3.35 us (2%)
    pallas_call x1, Pallas kernels, body(): call(act_loc[0].transpose(1, 2, 0, 3), w_loc[0].reshape(TAPS, LN, 1024),...  142 us
    broadcast_in_dim x1, other arithmetic, body(): z.transpose(2, 0, 1, 3)[None]  3.97 us
    unnamed x8, local copies, waits for them, and re-layouts  3.35 us

profile of v8, /device:TPU:4, one launch (start us, length us, event | category | flops | bytes accessed | tf_op | source)
XLA Modules:
  0.0 150.2 jit_solution(2331689184906277950)
XLA Ops:
  0.6 142.2 %conv_block.1 = (bf16[28,28,8,256]{3,2,1,0:T(8,128)(2,1)}, bf16[28,28,2,512]{3,2,1,0:T(2,128)(2,1)}, f32[9,128,1024]{2,1,0:T(8,128)}) custom-call(bf16[28,28,2,512]{3,2,1,0:T(2,128)(2,1)} %bitcast.21, bf16[9,128,1024]{2,1,0:T(8,128)(2,1)} %bitcast.19, f32[1,256]{1,0:T(1,128)} %sc.1, f32[1,256]{1,0:T(1,128)} %sh.1, bf16[28,28,8,256]{3,2,1,0:T(8,128)(2,1)} %bitcast.18), custom_call_target="tpu_custom_call" | custom-call | tf_op jit(solution)/shard_map/conv_block/pallas_call | solution.py:456
  142.8 0.0 slice-start
  142.8 0.0 copy-start
  142.8 0.0 slice-start.1
  142.9 4.0 %maximum_bitcast_fusion = bf16[1,8,28,28,256]{4,1,3,2,0:T(8,128)(2,1)} fusion(bf16[28,28,8,256]{3,2,1,0:T(8,128)(2,1)} %get-tuple-element.6), kind=kLoop, calls=%fused_computation | loop fusion | flops 1605632 | bytes 6422528 | tf_op jit(solution)/shard_map/broadcast_in_dim | solution.py:458
  146.8 0.0 copy-done
  146.8 1.2 copy.10
  148.0 0.0 slice-done
  148.0 0.0 slice-done.1
  148.0 2.2 %copy.11 = f32[1,3,3,128,1024]{4,3,2,1,0:T(8,128)} copy(f32[1,3,3,128,1024]{4,3,2,1,0:T(8,128)S(1)} %bitcast.17) | data formatting | bytes 9437184
  (1 shorter events, 0.0 us)
Async XLA Ops:
  142.8 5.2 %slice-start = ((s8[4718592]{0:T(1024)(128)(4,1)}), s8[4194304]{0:T(1024)(128)(4,1)S(1)}, s32[]{:S(2)}) async-start(s8[4718592]{0:T(1024)(128)(4,1)} %bitcast.15), calls=%async_computation | async-start | bytes 8388608
  142.8 4.0 %copy-start = (bf16[28,28,2,512]{3,2,1,0:T(2,128)(2,1)S(1)}, bf16[28,28,2,512]{3,2,1,0:T(2,128)(2,1)}, u32[]{:S(2)}) copy-start(bf16[28,28,2,512]{3,2,1,0:T(2,128)(2,1)} %get-tuple-element.7) | copy-start | bytes 4816900
  142.8 5.1 %slice-start.1 = ((s8[4718592]{0:T(1024)(128)(4,1)}), s8[524288]{0:T(1024)(128)(4,1)S(1)}, s32[]{:S(2)}) async-start(s8[4718592]{0:T(1024)(128)(4,1)} %bitcast.15), calls=%async_computation.1 | async-start | bytes 1048576
